TPU v7x, 32 devices: a whole 2x2x4 slice. The times are simulated.
32 devices in a mesh: blk: 8 (over y, x, core), uly: 4 (over z).
Axes of the slice: x: 2, y: 2, z: 4, core: 2. Of those that a mesh axis runs over, the one named last changes fastest.
Arguments:
- queries: bfloat16 [4096, 4096], P(('blk', 'uly')), may hold values from -100 to 100
- keys: bfloat16 [4096, 512], P(('blk', 'uly')), may hold values from -6 to 6
- values: bfloat16 [4096, 512], P(('blk', 'uly')), may hold values from -6 to 6
- segments: int32 [4096], P(('blk', 'uly')), may hold values from 0 to 7, never falling along the last dimension, each value on 1 to 2048 neighbouring positions
Outputs:
- attended: bfloat16 [4096, 4096], P(('blk', 'uly'))
Inputs may be any that keep to these rules, and one draw needn't show every extreme that they name: `segments`: document numbers never fall along the sequence; each document holds 1 to 2048 positions.
All inputs are finite; a program needn't handle non-finite values.
Results may differ from a plain program's by a relative error of at most 0.0039.
Values may be sent and summed in bfloat16 or wider, within the bound.
No kernel may reach another device: no remote copies, remote signals or barrier semaphores. Data moves between devices by JAX's collectives and lax.ppermute only.
A program may use at most 64 MiB of HBM per device.

v0:
```python
import jax
import jax.numpy as jnp
from jax import lax
from jax.sharding import PartitionSpec as P

HEAD_SIZE = 128


def update(state, qblk, qpos, qseg, kblk, vblk, kpos, kseg):
    top, total, accum = state
    scores = jnp.einsum(
        "qgpd,kgd->gpqk", qblk, kblk, preferred_element_type=jnp.float32
    ) * HEAD_SIZE ** (-0.5)
    allowed = (kpos[None, :] <= qpos[:, None]) & (kseg[None, :] == qseg[:, None])
    scores = jnp.where(allowed, scores, -1e30)
    fresh = jnp.maximum(top, jnp.max(scores, axis=-1))
    probs = jnp.where(allowed, jnp.exp(scores - fresh[..., None]), 0.0)
    factor = jnp.exp(top - fresh)
    total = total * factor + jnp.sum(probs, axis=-1)
    summed = jnp.einsum(
        "gpqk,kgd->qgpd", probs.astype(jnp.bfloat16), vblk, preferred_element_type=jnp.float32
    )
    accum = accum * jnp.transpose(factor, (2, 0, 1))[..., None] + summed
    return (fresh, total, accum)


def local(queries, keys, values, segments):
    qlocal, klocal, vlocal = (
        lax.all_to_all(queries, "uly", split_axis=1, concat_axis=0, tiled=True),
        lax.all_to_all(keys, "uly", split_axis=1, concat_axis=0, tiled=True),
        lax.all_to_all(values, "uly", split_axis=1, concat_axis=0, tiled=True),
    )
    everyone = lax.all_gather(segments, ("blk", "uly"), axis=0, tiled=True)
    rows = qlocal.shape[0]
    half = rows // 2
    head_groups = klocal.shape[1] // HEAD_SIZE
    per = qlocal.shape[1] // HEAD_SIZE // head_groups
    myself = lax.axis_index("blk")
    offsets = jnp.arange(half, dtype=jnp.int32)
    lower_q = qlocal[:half]
    upper_q = qlocal[half:]
    lower_pos = myself * rows + offsets
    upper_pos = myself * rows + half + offsets
    halves = []
    for qpart, qpos in ((lower_q, lower_pos), (upper_q, upper_pos)):
        qseg = lax.dynamic_slice_in_dim(everyone, qpos[0], half, 0)
        halves.append((qpart.reshape(half, head_groups, per, HEAD_SIZE), qpos, qseg))
    start_state = (
        jnp.full((head_groups, per, half), -1e30, jnp.float32),
        jnp.zeros((head_groups, per, half), jnp.float32),
        jnp.zeros((half, head_groups, per, HEAD_SIZE), jnp.float32),
    )
    carry = (start_state, start_state)
    kpiece = lax.all_gather(klocal, "blk", axis=0, tiled=True)
    vpiece = lax.all_gather(vlocal, "blk", axis=0, tiled=True)
    count = kpiece.shape[0]
    block = 512
    number = count // block
    kblocks = kpiece.reshape(number, block, head_groups, HEAD_SIZE)
    vblocks = vpiece.reshape(number, block, head_groups, HEAD_SIZE)
    firsts = jnp.arange(number, dtype=jnp.int32) * block

    def visit(state, item):
        kblk, vblk, first = item
        kpos = first + jnp.arange(block, dtype=jnp.int32)
        kseg = lax.dynamic_slice_in_dim(everyone, first, block, 0)
        final_output = []
        for index in range(2):
            qblk, qpos, qseg = halves[index]
            final_output.append(
                lax.cond(
                    first <= qpos[-1],
                    lambda s: update(s, qblk, qpos, qseg, kblk, vblk, kpos, kseg),
                    lambda s: s,
                    state[index],
                )
            )
        return (tuple(final_output), None)

    carry, unused = lax.scan(visit, carry, (kblocks, vblocks, firsts))
    outputs = []
    for state in carry:
        top, total, accum = state
        normed = accum / jnp.transpose(total, (2, 0, 1))[..., None]
        outputs.append(normed.reshape(half, head_groups * per * HEAD_SIZE).astype(jnp.bfloat16))
    lower_out, upper_out = outputs
    joined = jnp.concatenate([lower_out, upper_out], axis=0)
    return lax.all_to_all(joined, "uly", split_axis=0, concat_axis=1, tiled=True)


def solution(mesh):
    in_specs = (
        P(("blk", "uly"), None),
        P(("blk", "uly"), None),
        P(("blk", "uly"), None),
        P(("blk", "uly")),
    )
    out_specs = P(("blk", "uly"), None)
    return jax.shard_map(local, mesh=mesh, in_specs=in_specs, out_specs=out_specs, check_vma=False)
```

profile of v0, /device:TPU:7, one launch (start us, length us, event | category | flops | bytes accessed | tf_op | source)
XLA Modules:
  0.0 264.4 jit_solution(7177814763644363168)
XLA Ops:
  7.7 9.3 %all_to_all.73 = bf16[128,4,128]{2,0,1:T(8,128)(2,1)} all-to-all(bf16[128,4,128]{2,0,1:T(8,128)(2,1)S(1)} %copy.44), channel_id=1, replica_groups=mesh['blk'=8,'uly'=4] {'uly'}, dimensions={1} | all-to-all | bytes 262144 | tf_op jit(solution)/shard_map/all_to_all | solution.py:30
  18.8 3.5 %all-to-all-start.1 = ((bf16[128,4,128]{2,0,1:T(8,128)(2,1)}), bf16[128,4,128]{2,0,1:T(8,128)(2,1)S(1)}, u32[]{:S(2)}, u32[]{:S(2)}) async-start(bf16[128,4,128]{2,0,1:T(8,128)(2,1)} %copy.46), calls=%async_computation.1 | async-start | bytes 262144 | tf_op jit(solution)/shard_map/all_to_all | solution.py:31
  22.3 2.3 copy.61
  24.6 2.5 all-to-all-done.1
  27.1 3.5 %all-to-all-start.2 = ((bf16[128,4,1024]{2,0,1:T(8,128)(2,1)}), bf16[128,4,1024]{2,0,1:T(8,128)(2,1)S(1)}, u32[]{:S(2)}, u32[]{:S(2)}) async-start(bf16[128,4,1024]{2,0,1:T(8,128)(2,1)} %bitcast.164), calls=%async_computation.2 | async-start | bytes 2097152 | tf_op jit(solution)/shard_map/all_to_all | solution.py:29
  36.1 68.5 %all-gather = s32[32,1,128]{2,1,0:T(1,128)S(1)} all-gather(s32[1,1,128]{2,1,0:T(1,128)S(1)} %bitcast.198), channel_id=1, replica_groups=mesh['blk'=8,'uly'=4] {'blk','uly'}, dimensions={0}, use_global_device_ids=true | all-gather | bytes 16896 | tf_op jit(solution)/shard_map/all_gather | solution.py:33
  105.3 121.5 %while.20 = (s32[]{:T(128)}, f32[1,8,256]{2,1,0:T(8,128)S(1)}, f32[1,8,256]{2,1,0:T(8,128)S(1)}, f32[256,1,8,128]{3,0,2,1:T(8,128)S(1)}, f32[1,8,256]{2,1,0:T(8,...) while((s32[]{:T(128)}, f32[1,8,256]{2,1,0:T(8,128)S(1)}, ...), condition=%wide.region_9.10_spmd, body=%wide.region_0.9_spmd.sunk | while | flops 1102852608 | bytes 32786988 | solution.py:80
  111.4 3.7 %conditional.5 = ((f32[1,8,256]{2,1,0:T(8,128)S(1)}, f32[1,8,256]{2,1,0:T(8,128)S(1)}, f32[256,1,8,128]{3,0,2,1:T(8,128)S(1)})) conditional(s32[]{:T(128)} %convert_element_type.49, (f32[1,8,256]{2,1,0:T(8,128)S(1)}, f32[1,8,256]{2,1,0:T(8,128)S(1)}, f32[256,1,8,128]{3,0,2,1:T(8,128)S(1)}) %tuple.52, (s32[512]{0:T(512)S(1)}, s32[256]{0:T(256)S(1)}, ...), branch_computations={%region_5.5_spmd, %region_6.8_spmd} | conditional | flops 551426048 | bytes 16128032 | solution.py:71
  116.9 3.7 %conditional.4 = ((f32[1,8,256]{2,1,0:T(8,128)S(1)}, f32[1,8,256]{2,1,0:T(8,128)S(1)}, f32[256,1,8,128]{3,0,2,1:T(8,128)S(1)})) conditional(s32[]{:T(128)} %convert_element_type.48, (f32[1,8,256]{2,1,0:T(8,128)S(1)}, f32[1,8,256]{2,1,0:T(8,128)S(1)}, f32[256,1,8,128]{3,0,2,1:T(8,128)S(1)}) %tuple.50, (s32[512]{0:T(512)S(1)}, s32[256]{0:T(256)S(1)}, ...), branch_computations={%region_1.1_spmd, %region_2.4_spmd} | conditional | flops 551426048 | bytes 16128032 | solution.py:71
  126.6 3.7 %conditional.5 = ((f32[1,8,256]{2,1,0:T(8,128)S(1)}, f32[1,8,256]{2,1,0:T(8,128)S(1)}, f32[256,1,8,128]{3,0,2,1:T(8,128)S(1)})) conditional(s32[]{:T(128)} %convert_element_type.49, (f32[1,8,256]{2,1,0:T(8,128)S(1)}, f32[1,8,256]{2,1,0:T(8,128)S(1)}, f32[256,1,8,128]{3,0,2,1:T(8,128)S(1)}) %tuple.52, (s32[512]{0:T(512)S(1)}, s32[256]{0:T(256)S(1)}, ...), branch_computations={%region_5.5_spmd, %region_6.8_spmd} | conditional | flops 551426048 | bytes 16128032 | solution.py:71
  132.1 3.7 %conditional.4 = ((f32[1,8,256]{2,1,0:T(8,128)S(1)}, f32[1,8,256]{2,1,0:T(8,128)S(1)}, f32[256,1,8,128]{3,0,2,1:T(8,128)S(1)})) conditional(s32[]{:T(128)} %convert_element_type.48, (f32[1,8,256]{2,1,0:T(8,128)S(1)}, f32[1,8,256]{2,1,0:T(8,128)S(1)}, f32[256,1,8,128]{3,0,2,1:T(8,128)S(1)}) %tuple.50, (s32[512]{0:T(512)S(1)}, s32[256]{0:T(256)S(1)}, ...), branch_computations={%region_1.1_spmd, %region_2.4_spmd} | conditional | flops 551426048 | bytes 16128032 | solution.py:71
  141.8 3.7 %conditional.5 = ((f32[1,8,256]{2,1,0:T(8,128)S(1)}, f32[1,8,256]{2,1,0:T(8,128)S(1)}, f32[256,1,8,128]{3,0,2,1:T(8,128)S(1)})) conditional(s32[]{:T(128)} %convert_element_type.49, (f32[1,8,256]{2,1,0:T(8,128)S(1)}, f32[1,8,256]{2,1,0:T(8,128)S(1)}, f32[256,1,8,128]{3,0,2,1:T(8,128)S(1)}) %tuple.52, (s32[512]{0:T(512)S(1)}, s32[256]{0:T(256)S(1)}, ...), branch_computations={%region_5.5_spmd, %region_6.8_spmd} | conditional | flops 551426048 | bytes 16128032 | solution.py:71
  147.2 3.7 %conditional.4 = ((f32[1,8,256]{2,1,0:T(8,128)S(1)}, f32[1,8,256]{2,1,0:T(8,128)S(1)}, f32[256,1,8,128]{3,0,2,1:T(8,128)S(1)})) conditional(s32[]{:T(128)} %convert_element_type.48, (f32[1,8,256]{2,1,0:T(8,128)S(1)}, f32[1,8,256]{2,1,0:T(8,128)S(1)}, f32[256,1,8,128]{3,0,2,1:T(8,128)S(1)}) %tuple.50, (s32[512]{0:T(512)S(1)}, s32[256]{0:T(256)S(1)}, ...), branch_computations={%region_1.1_spmd, %region_2.4_spmd} | conditional | flops 551426048 | bytes 16128032 | solution.py:71
  157.0 3.7 %conditional.5 = ((f32[1,8,256]{2,1,0:T(8,128)S(1)}, f32[1,8,256]{2,1,0:T(8,128)S(1)}, f32[256,1,8,128]{3,0,2,1:T(8,128)S(1)})) conditional(s32[]{:T(128)} %convert_element_type.49, (f32[1,8,256]{2,1,0:T(8,128)S(1)}, f32[1,8,256]{2,1,0:T(8,128)S(1)}, f32[256,1,8,128]{3,0,2,1:T(8,128)S(1)}) %tuple.52, (s32[512]{0:T(512)S(1)}, s32[256]{0:T(256)S(1)}, ...), branch_computations={%region_5.5_spmd, %region_6.8_spmd} | conditional | flops 551426048 | bytes 16128032 | solution.py:71
  162.4 3.7 %conditional.4 = ((f32[1,8,256]{2,1,0:T(8,128)S(1)}, f32[1,8,256]{2,1,0:T(8,128)S(1)}, f32[256,1,8,128]{3,0,2,1:T(8,128)S(1)})) conditional(s32[]{:T(128)} %convert_element_type.48, (f32[1,8,256]{2,1,0:T(8,128)S(1)}, f32[1,8,256]{2,1,0:T(8,128)S(1)}, f32[256,1,8,128]{3,0,2,1:T(8,128)S(1)}) %tuple.50, (s32[512]{0:T(512)S(1)}, s32[256]{0:T(256)S(1)}, ...), branch_computations={%region_1.1_spmd, %region_2.4_spmd} | conditional | flops 551426048 | bytes 16128032 | solution.py:71
  172.2 3.7 %conditional.5 = ((f32[1,8,256]{2,1,0:T(8,128)S(1)}, f32[1,8,256]{2,1,0:T(8,128)S(1)}, f32[256,1,8,128]{3,0,2,1:T(8,128)S(1)})) conditional(s32[]{:T(128)} %convert_element_type.49, (f32[1,8,256]{2,1,0:T(8,128)S(1)}, f32[1,8,256]{2,1,0:T(8,128)S(1)}, f32[256,1,8,128]{3,0,2,1:T(8,128)S(1)}) %tuple.52, (s32[512]{0:T(512)S(1)}, s32[256]{0:T(256)S(1)}, ...), branch_computations={%region_5.5_spmd, %region_6.8_spmd} | conditional | flops 551426048 | bytes 16128032 | solution.py:71
  177.6 3.7 %conditional.4 = ((f32[1,8,256]{2,1,0:T(8,128)S(1)}, f32[1,8,256]{2,1,0:T(8,128)S(1)}, f32[256,1,8,128]{3,0,2,1:T(8,128)S(1)})) conditional(s32[]{:T(128)} %convert_element_type.48, (f32[1,8,256]{2,1,0:T(8,128)S(1)}, f32[1,8,256]{2,1,0:T(8,128)S(1)}, f32[256,1,8,128]{3,0,2,1:T(8,128)S(1)}) %tuple.50, (s32[512]{0:T(512)S(1)}, s32[256]{0:T(256)S(1)}, ...), branch_computations={%region_1.1_spmd, %region_2.4_spmd} | conditional | flops 551426048 | bytes 16128032 | solution.py:71
  187.4 3.7 %conditional.5 = ((f32[1,8,256]{2,1,0:T(8,128)S(1)}, f32[1,8,256]{2,1,0:T(8,128)S(1)}, f32[256,1,8,128]{3,0,2,1:T(8,128)S(1)})) conditional(s32[]{:T(128)} %convert_element_type.49, (f32[1,8,256]{2,1,0:T(8,128)S(1)}, f32[1,8,256]{2,1,0:T(8,128)S(1)}, f32[256,1,8,128]{3,0,2,1:T(8,128)S(1)}) %tuple.52, (s32[512]{0:T(512)S(1)}, s32[256]{0:T(256)S(1)}, ...), branch_computations={%region_5.5_spmd, %region_6.8_spmd} | conditional | flops 551426048 | bytes 16128032 | solution.py:71
  192.8 3.7 %conditional.4 = ((f32[1,8,256]{2,1,0:T(8,128)S(1)}, f32[1,8,256]{2,1,0:T(8,128)S(1)}, f32[256,1,8,128]{3,0,2,1:T(8,128)S(1)})) conditional(s32[]{:T(128)} %convert_element_type.48, (f32[1,8,256]{2,1,0:T(8,128)S(1)}, f32[1,8,256]{2,1,0:T(8,128)S(1)}, f32[256,1,8,128]{3,0,2,1:T(8,128)S(1)}) %tuple.50, (s32[512]{0:T(512)S(1)}, s32[256]{0:T(256)S(1)}, ...), branch_computations={%region_1.1_spmd, %region_2.4_spmd} | conditional | flops 551426048 | bytes 16128032 | solution.py:71
  202.6 3.7 %conditional.5 = ((f32[1,8,256]{2,1,0:T(8,128)S(1)}, f32[1,8,256]{2,1,0:T(8,128)S(1)}, f32[256,1,8,128]{3,0,2,1:T(8,128)S(1)})) conditional(s32[]{:T(128)} %convert_element_type.49, (f32[1,8,256]{2,1,0:T(8,128)S(1)}, f32[1,8,256]{2,1,0:T(8,128)S(1)}, f32[256,1,8,128]{3,0,2,1:T(8,128)S(1)}) %tuple.52, (s32[512]{0:T(512)S(1)}, s32[256]{0:T(256)S(1)}, ...), branch_computations={%region_5.5_spmd, %region_6.8_spmd} | conditional | flops 551426048 | bytes 16128032 | solution.py:71
  208.0 3.7 %conditional.4 = ((f32[1,8,256]{2,1,0:T(8,128)S(1)}, f32[1,8,256]{2,1,0:T(8,128)S(1)}, f32[256,1,8,128]{3,0,2,1:T(8,128)S(1)})) conditional(s32[]{:T(128)} %convert_element_type.48, (f32[1,8,256]{2,1,0:T(8,128)S(1)}, f32[1,8,256]{2,1,0:T(8,128)S(1)}, f32[256,1,8,128]{3,0,2,1:T(8,128)S(1)}) %tuple.50, (s32[512]{0:T(512)S(1)}, s32[256]{0:T(256)S(1)}, ...), branch_computations={%region_1.1_spmd, %region_2.4_spmd} | conditional | flops 551426048 | bytes 16128032 | solution.py:71
  217.8 3.7 %conditional.5 = ((f32[1,8,256]{2,1,0:T(8,128)S(1)}, f32[1,8,256]{2,1,0:T(8,128)S(1)}, f32[256,1,8,128]{3,0,2,1:T(8,128)S(1)})) conditional(s32[]{:T(128)} %convert_element_type.49, (f32[1,8,256]{2,1,0:T(8,128)S(1)}, f32[1,8,256]{2,1,0:T(8,128)S(1)}, f32[256,1,8,128]{3,0,2,1:T(8,128)S(1)}) %tuple.52, (s32[512]{0:T(512)S(1)}, s32[256]{0:T(256)S(1)}, ...), branch_computations={%region_5.5_spmd, %region_6.8_spmd} | conditional | flops 551426048 | bytes 16128032 | solution.py:71
  223.2 3.7 %conditional.4 = ((f32[1,8,256]{2,1,0:T(8,128)S(1)}, f32[1,8,256]{2,1,0:T(8,128)S(1)}, f32[256,1,8,128]{3,0,2,1:T(8,128)S(1)})) conditional(s32[]{:T(128)} %convert_element_type.48, (f32[1,8,256]{2,1,0:T(8,128)S(1)}, f32[1,8,256]{2,1,0:T(8,128)S(1)}, f32[256,1,8,128]{3,0,2,1:T(8,128)S(1)}) %tuple.50, (s32[512]{0:T(512)S(1)}, s32[256]{0:T(256)S(1)}, ...), branch_computations={%region_1.1_spmd, %region_2.4_spmd} | conditional | flops 551426048 | bytes 16128032 | solution.py:71
  230.6 25.0 %all_to_all.74 = bf16[4,128,1024]{2,1,0:T(8,128)(2,1)S(1)} all-to-all(bf16[4,128,1024]{2,1,0:T(8,128)(2,1)S(1)} %bitcast.174), channel_id=1, replica_groups=mesh['blk'=8,'uly'=4] {'uly'}, dimensions={0} | all-to-all | bytes 2097152 | tf_op jit(solution)/shard_map/all_to_all | solution.py:88
  (199 shorter events, 96.3 us)
Async XLA Ops:
  6.5 29.5 %copy-start.1 = (s32[128]{0:T(128)S(1)}, s32[128]{0:T(128)}, u32[]{:S(2)}) copy-start(s32[128]{0:T(128)} %param.13) | copy-start | bytes 1540
  6.5 98.6 %all-gather.4.cloned.1.call-start = ((), (), s32[]{:S(2)}) async-start(), calls=%async_computation.4 | async-start | bytes 1179648 | tf_op jit(solution)/shard_map/all_gather | solution.py:54
  18.8 8.3 %all-to-all-start.1 = ((bf16[128,4,128]{2,0,1:T(8,128)(2,1)}), bf16[128,4,128]{2,0,1:T(8,128)(2,1)S(1)}, u32[]{:S(2)}, u32[]{:S(2)}) async-start(bf16[128,4,128]{2,0,1:T(8,128)(2,1)} %copy.46), calls=%async_computation.1 | async-start | bytes 262144 | tf_op jit(solution)/shard_map/all_to_all | solution.py:31
  27.1 3.6 %copy-start = (bf16[128,4,128]{2,0,1:T(8,128)(2,1)}, bf16[128,4,128]{2,0,1:T(8,128)(2,1)S(1)}, u32[]{:S(2)}) copy-start(bf16[128,4,128]{2,0,1:T(8,128)(2,1)S(1)} %all-to-all-done.1) | copy-start | bytes 393220
  27.1 77.6 %all-to-all-start.2 = ((bf16[128,4,1024]{2,0,1:T(8,128)(2,1)}), bf16[128,4,1024]{2,0,1:T(8,128)(2,1)S(1)}, u32[]{:S(2)}, u32[]{:S(2)}) async-start(bf16[128,4,1024]{2,0,1:T(8,128)(2,1)} %bitcast.164), calls=%async_computation.2 | async-start | bytes 2097152 | tf_op jit(solution)/shard_map/all_to_all | solution.py:29
  30.6 74.5 %all-gather.6.cloned.1.call-start = ((), (), s32[]{:S(2)}) async-start(), calls=%async_computation.5 | async-start | bytes 1179648 | tf_op jit(solution)/shard_map/all_gather | solution.py:55
Sparse Core Ops, SparseCore 0:
  17.1 23.4 all-gather.3
  42.5 23.3 all-gather.5
where the time goes:
time: 266 us; the launch traced here: 264 us
  blocking collectives  103 us (39%)
  matrix products  37.8 us (14%)
  loops' own time  36.4 us (14%)
  local copies, waits for them, and re-layouts  33.6 us (13%)
  other arithmetic  26.4 us (10%)
  between operations  17.2 us (6%)
  starting transfers between devices  7.06 us (3%)
  waiting for transfers between devices  3.23 us (1%)
    all_gather x1, blocking collectives, local(): everyone = lax.all_gather(segments, ('blk', 'uly'), axis=0, tiled=True)  68.5 us
    another operation x1, loops' own time, local(): carry, unused = lax.scan(visit, carry, (kblocks, vblocks, firsts))  35.3 us
    dot_general x16, matrix products, update(): jnp.einsum('gpqk,kgd->qgpd', probs.astype(jnp.bfloat16), vblk, preferred_...  25.1 us
    all_to_all x1, blocking collectives, local(): lax.all_to_all(joined, 'uly', split_axis=0, concat_axis=1, tiled=True)  25 us
    reduce_sum x16, other arithmetic, update(): total = total * factor + jnp.sum(probs, axis=-1)  16.1 us
    dot_general x16, matrix products, update(): jnp.einsum('qgpd,kgd->gpqk', qblk, kblk, preferred_element_type=jnp.float32)  12.7 us
    all_to_all x1, blocking collectives, local(): lax.all_to_all(keys, 'uly', split_axis=1, concat_axis=0, tiled=True)  9.27 us
    slice x16, local copies, waits for them, and re-layouts, visit(): qpos[-1]  9.2 us
  transfers between devices with their start and end apart: 4, of which 1 were waited for; matrix products, arithmetic and copies ran while one was open for 2% of the time, Pallas kernels for 0%

commit v1 on v0

v1 whole, which is shorter than its diff:
```python
import functools

import jax
import jax.numpy as jnp
from jax import lax
from jax.experimental import pallas as pl
from jax.experimental.pallas import tpu as pltpu
from jax.sharding import Mesh
from jax.sharding import PartitionSpec as P

HEAD_SIZE = 128
LOG2E = 1.4426950408889634
LOW = -1e30


def attend(where, q_ref, own_ref, mate_ref, out_ref, s_ref, p_ref, m_ref, l_ref, acc_ref, *, rows, layers, split):
    groups, _, width = q_ref.shape
    per = width // HEAD_SIZE
    sources = own_ref.shape[0]
    block = layers * rows
    scale = HEAD_SIZE ** -0.5 * LOG2E
    chip0, core, layer = where[0], where[1], where[2]

    counts = jnp.zeros((8, HEAD_SIZE), jnp.float32)
    for ref in (own_ref, mate_ref):
        for i in range(sources):
            counts = counts + ref[i, 2 * rows :, :].astype(jnp.float32)
    ends = counts[:1]

    part = per // split
    for g in range(groups):
        blk = (chip0 + g) * 2 + core
        first = (blk * layers + layer) * rows
        place = first + lax.broadcasted_iota(jnp.int32, (rows, 1), 0)
        placef = place.astype(jnp.float32)
        start = jnp.max(jnp.where(ends <= placef, ends, 0.0), axis=1, keepdims=True).astype(jnp.int32)
        low = jnp.min(start)
        low_blk = low // block
        m_ref[...] = jnp.full(m_ref.shape, LOW, jnp.float32)
        l_ref[...] = jnp.zeros(l_ref.shape, jnp.float32)
        acc_ref[...] = jnp.zeros(acc_ref.shape, jnp.float32)

        def step(ref, chip, parity):
            base = (chip * 2 + parity) * block
            k = jnp.concatenate([ref[chip * layers + z, :rows, :] for z in range(layers)], axis=0)
            v = jnp.concatenate([ref[chip * layers + z, rows : 2 * rows, :] for z in range(layers)], axis=0)
            key = base + lax.broadcasted_iota(jnp.int32, (rows, block), 1)
            bias = jnp.where((key <= place) & (key >= start), 0.0, LOW)
            for h0 in range(0, per, part):
                q = jnp.concatenate(
                    [q_ref[g, :, h * HEAD_SIZE : (h + 1) * HEAD_SIZE] for h in range(h0, h0 + part)], axis=0
                )
                s = lax.dot_general(q, k, (((1,), (1,)), ((), ())), preferred_element_type=jnp.float32)
                ps = []
                factors = []
                for i in range(part):
                    r = pl.ds((h0 + i) * rows, rows)
                    x = s[i * rows : (i + 1) * rows] * scale + bias
                    old = m_ref[r, :]
                    top = jnp.maximum(old, jnp.max(x, axis=1, keepdims=True))
                    p = jnp.exp2(x - top[:, :1])
                    factor = jnp.exp2(old - top)
                    m_ref[r, :] = top
                    l_ref[r, :] = l_ref[r, :] * factor + jnp.sum(p, axis=1, keepdims=True)
                    ps.append(p.astype(jnp.bfloat16))
                    factors.append(factor)
                pv = lax.dot_general(
                    jnp.concatenate(ps, axis=0), v, (((1,), (0,)), ((), ())), preferred_element_type=jnp.float32
                )
                r = pl.ds(h0 * rows, part * rows)
                acc_ref[r, :] = acc_ref[r, :] * jnp.concatenate(factors, axis=0) + pv

        @pl.loop((low_blk - core + 1) // 2, chip0 + g + 1)
        def _(chip):
            step(own_ref, chip, core)

        other = 1 - core

        @pl.loop((low_blk - other + 1) // 2, (blk - other) // 2 + 1)
        def _(chip):
            step(mate_ref, chip, other)

        for h in range(per):
            r = pl.ds(h * rows, rows)
            out_ref[g, :, h * HEAD_SIZE : (h + 1) * HEAD_SIZE] = (acc_ref[r, :] / l_ref[r, :]).astype(out_ref.dtype)


def local(queries, keys, values, segments, *, outer, groups, layers):
    rows = queries.shape[0]
    per_head = queries.shape[1] // groups
    per = per_head // HEAD_SIZE
    members = outer * groups * layers
    below = (segments[:, None] < jnp.arange(HEAD_SIZE, dtype=jnp.int32)[None, :]).astype(jnp.float32)
    counts = jnp.broadcast_to(jnp.sum(below, axis=0)[None, :], (8, HEAD_SIZE)).astype(jnp.bfloat16)

    q = lax.all_to_all(
        queries.reshape(rows, groups, per_head).swapaxes(0, 1), "group", split_axis=0, concat_axis=0, tiled=True
    )
    kv = jnp.concatenate(
        [
            keys.reshape(rows, groups, HEAD_SIZE).swapaxes(0, 1),
            values.reshape(rows, groups, HEAD_SIZE).swapaxes(0, 1),
            jnp.broadcast_to(counts[None], (groups, 8, HEAD_SIZE)),
        ],
        axis=1,
    )
    piece = kv.shape[1]
    sent = jnp.broadcast_to(kv[None, :, None], (outer, groups, layers, piece, HEAD_SIZE))
    own = lax.all_to_all(
        sent.reshape(members, piece, HEAD_SIZE), ("outer", "group", "uly"), split_axis=0, concat_axis=0, tiled=True
    )
    mate = lax.ppermute(own, "core", [(0, 1), (1, 0)])
    where = jnp.stack(
        [lax.axis_index("outer") * groups, lax.axis_index("core"), lax.axis_index("uly")]
    ).astype(jnp.int32)
    block = layers * rows
    vmem = pl.BlockSpec(memory_space=pltpu.VMEM)
    out = pl.pallas_call(
        functools.partial(attend, rows=rows, layers=layers, split=2),
        out_shape=jax.ShapeDtypeStruct((groups, rows, per_head), jnp.bfloat16),
        in_specs=[pl.BlockSpec(memory_space=pltpu.SMEM), vmem, vmem, vmem],
        out_specs=vmem,
        scratch_shapes=[
            pltpu.VMEM((8, HEAD_SIZE), jnp.float32),
            pltpu.VMEM((16, HEAD_SIZE), jnp.bfloat16),
            pltpu.VMEM((per * rows, HEAD_SIZE), jnp.float32),
            pltpu.VMEM((per * rows, HEAD_SIZE), jnp.float32),
            pltpu.VMEM((per * rows, HEAD_SIZE), jnp.float32),
        ],
        name="attend",
    )(where, q, own, mate)
    back = lax.all_to_all(out, "group", split_axis=0, concat_axis=0, tiled=True)
    return back.swapaxes(0, 1).reshape(rows, groups * per_head)


def solution(mesh):
    blocks, layers = mesh.shape["blk"], mesh.shape["uly"]

    def run(queries, keys, values, segments):
        groups = keys.shape[1] // HEAD_SIZE
        outer = blocks // 2 // groups
        fine = Mesh(mesh.devices.reshape(outer, groups, 2, layers), ("outer", "group", "core", "uly"))
        axes = ("outer", "group", "core", "uly")
        body = functools.partial(local, outer=outer, groups=groups, layers=layers)
        return jax.shard_map(
            body, mesh=fine, in_specs=(P(axes), P(axes), P(axes), P(axes)), out_specs=P(axes), check_vma=False
        )(queries, keys, values, segments)

    return run
```

time: 266 us -> 98.1 us (0.37)
  the two profiles are of different devices: /device:TPU:7 before, /device:TPU:1 now
where the time goes in v1:
time: 98.1 us; the launch traced here: 96.3 us
  blocking collectives  50 us (51%)
  Pallas kernels  17.8 us (18%)
  waiting for transfers between devices  12.7 us (13%)
  local copies, waits for them, and re-layouts  8.97 us (9%)
  starting transfers between devices  5.21 us (5%)
  other arithmetic  1.54 us (2%)
    all_to_all x1, blocking collectives, local(): lax.all_to_all(sent.reshape(members, piece, HEAD_SIZE), ('outer', 'group'...  34.6 us
    pallas_call x1, Pallas kernels, local(): pl.pallas_call(functools.partial(attend, rows=rows, layers=layers, split=...  17.8 us
    all_to_all x1, blocking collectives, local(): back = lax.all_to_all(out, 'group', split_axis=0, concat_axis=0, tiled=True)  15.4 us
    all_to_all x1, waiting for transfers between devices, local(): lax.all_to_all(queries.reshape(rows, groups, per_head).swapaxes(0, 1), 'g...  12.7 us
    unnamed x7, local copies, waits for them, and re-layouts  3.62 us
    all_to_all x1, starting transfers between devices, local(): lax.all_to_all(queries.reshape(rows, groups, per_head).swapaxes(0, 1), 'g...  3.52 us
  transfers between devices with their start and end apart: 2, of which 1 were waited for; matrix products, arithmetic and copies ran while one was open for 4% of the time, Pallas kernels for 0%

profile of v1, /device:TPU:1, one launch (start us, length us, event | category | flops | bytes accessed | tf_op | source)
XLA Modules:
  0.0 96.3 jit_solution(3854728692293328567)
XLA Ops:
  0.0 0.8 convert_reduce_fusion
  0.8 0.9 reshape.20
  1.7 0.9 reshape.21
  2.7 0.2 pad_maximum_fusion
  2.9 0.1 broadcast_in_dim.7
  3.1 34.6 %all_to_all.15.own_ref = bf16[16,264,128]{2,1,0:T(8,128)(2,1)S(1)} all-to-all(bf16[16,264,128]{2,1,0:T(8,128)(2,1)S(1)} %bitcast.9), channel_id=1, replica_groups=mesh['outer'=1,'group'=4,'core'=2,'uly'=4] {'outer','group','uly'}, dimensions={0} | all-to-all | bytes 2162688 | tf_op jit(solution)/shard_map/all_to_all | solution.py:109
  37.7 0.0 copy-start
  37.7 1.7 %collective-permute-start = (bf16[16,264,128]{2,1,0:T(8,128)(2,1)S(1)}, bf16[16,264,128]{2,1,0:T(8,128)(2,1)S(1)}, u32[]{:S(2)}, u32[]{:S(2)}) collective-permute-start(bf16[16,264,128]{2,1,0:T(8,128)(2,1)S(1)} %all_to_all.15.own_ref), channel_id=1, source_target_pairs={{0,4},{4,0},{1,5},{5,1},{2,6},{6,2},{3,7},{7,3},{8,12},{12,8},{9,1... | collective-permute-start | bytes 3244040 | tf_op jit(solution)/shard_map/ppermute | solution.py:112
  39.3 1.6 %copy.11 = bf16[128,4096]{0,1:T(8,128)(2,1)S(1)} copy(bf16[128,4096]{1,0:T(8,128)(2,1)} %param.4) | data formatting | bytes 2097152 | tf_op args[0]
  41.0 1.3 %copy.12 = bf16[128,4,1024]{2,0,1:T(8,128)(2,1)} copy(bf16[128,4,1024]{0,2,1:T(8,128)(2,1)S(1)} %bitcast.12) | data formatting | bytes 2097152 | tf_op jit(solution)/shard_map/reshape | solution.py:97
  42.3 0.0 copy-done
  42.3 3.5 %all-to-all-start = ((bf16[4,128,1024]{2,1,0:T(8,128)(2,1)}), bf16[4,128,1024]{2,1,0:T(8,128)(2,1)S(1)}, u32[]{:S(2)}, u32[]{:S(2)}) async-start(bf16[4,128,1024]{2,1,0:T(8,128)(2,1)} %bitcast.3), calls=%async_computation | async-start | bytes 2097152 | tf_op jit(solution)/shard_map/all_to_all | solution.py:96
  45.8 0.6 pad_add_fusion.where
  46.4 12.7 %all-to-all-done.q_ref = bf16[4,128,1024]{2,1,0:T(8,128)(2,1)S(1)} async-done(((bf16[4,128,1024]{2,1,0:T(8,128)(2,1)}), bf16[4,128,1024]{2,1,0:T(8,128)(2,1)S(1)}, u32[]{:S(2)}, u32[]{:S(2)}) %all-to-all-start) | async-done | bytes 1048608 | tf_op jit(solution)/shard_map/all_to_all | solution.py:96
  59.1 0.0 copy-start.1
  59.1 0.0 collective-permute-done.mate_ref
  59.1 1.0 %copy-done.1 = bf16[4,128,1024]{2,1,0:T(8,128)(2,1)} copy-done((bf16[4,128,1024]{2,1,0:T(8,128)(2,1)}, bf16[4,128,1024]{2,1,0:T(8,128)(2,1)S(1)}, u32[]{:S(2)}) %copy-start.1) | copy-done | bytes 1048600
  60.1 0.0 copy-start.2
  60.1 1.0 %copy-done.2 = bf16[16,264,128]{2,1,0:T(8,128)(2,1)} copy-done((bf16[16,264,128]{2,1,0:T(8,128)(2,1)}, bf16[16,264,128]{2,1,0:T(8,128)(2,1)S(1)}, u32[]{:S(2)}) %copy-start.2) | copy-done | bytes 1081368
  61.2 17.8 %attend.1 = bf16[4,128,1024]{2,1,0:T(8,128)(2,1)} custom-call(s32[3]{0:T(128)} %pad_add_fusion.where, bf16[4,128,1024]{2,1,0:T(8,128)(2,1)} %copy-done.1, bf16[16,264,128]{2,1,0:T(8,128)(2,1)} %copy-done, bf16[16,264,128]{2,1,0:T(8,128)(2,1)} %copy-done.2), custom_call_target="tpu_custom_call" | custom-call | tf_op jit(solution)/shard_map/attend/pallas_call | solution.py:118
  79.0 15.4 %all_to_all.16 = bf16[4,128,1024]{2,1,0:T(8,128)(2,1)S(1)} all-to-all(bf16[4,128,1024]{2,1,0:T(8,128)(2,1)} %attend.1), channel_id=1, replica_groups=mesh['outer'=1,'group'=4,'core'=2,'uly'=4] {'group'}, dimensions={0} | all-to-all | bytes 2097152 | tf_op jit(solution)/shard_map/all_to_all | solution.py:132
  94.3 0.7 copy.14
  95.0 1.3 %copy.15 = bf16[128,4096]{1,0:T(8,128)(2,1)} copy(bf16[128,4096]{0,1:T(8,128)(2,1)S(1)} %bitcast.11) | data formatting | bytes 2097152 | tf_op jit(solution)/shard_map/reshape | solution.py:133
  (2 shorter events, 0.0 us)
Async XLA Ops:
  37.7 4.6 %copy-start = (bf16[16,264,128]{2,1,0:T(8,128)(2,1)}, bf16[16,264,128]{2,1,0:T(8,128)(2,1)S(1)}, u32[]{:S(2)}) copy-start(bf16[16,264,128]{2,1,0:T(8,128)(2,1)S(1)} %all_to_all.15.own_ref) | copy-start | bytes 3244036
  37.7 21.5 %collective-permute-start = (bf16[16,264,128]{2,1,0:T(8,128)(2,1)S(1)}, bf16[16,264,128]{2,1,0:T(8,128)(2,1)S(1)}, u32[]{:S(2)}, u32[]{:S(2)}) collective-permute-start(bf16[16,264,128]{2,1,0:T(8,128)(2,1)S(1)} %all_to_all.15.own_ref), channel_id=1, source_target_pairs={{0,4},{4,0},{1,5},{5,1},{2,6},{6,2},{3,7},{7,3},{8,12},{12,8},{9,1... | collective-permute-start | bytes 3244040 | tf_op jit(solution)/shard_map/ppermute | solution.py:112
  42.3 16.9 %all-to-all-start = ((bf16[4,128,1024]{2,1,0:T(8,128)(2,1)}), bf16[4,128,1024]{2,1,0:T(8,128)(2,1)S(1)}, u32[]{:S(2)}, u32[]{:S(2)}) async-start(bf16[4,128,1024]{2,1,0:T(8,128)(2,1)} %bitcast.3), calls=%async_computation | async-start | bytes 2097152 | tf_op jit(solution)/shard_map/all_to_all | solution.py:96
  59.1 1.0 %copy-start.1 = (bf16[4,128,1024]{2,1,0:T(8,128)(2,1)}, bf16[4,128,1024]{2,1,0:T(8,128)(2,1)S(1)}, u32[]{:S(2)}) copy-start(bf16[4,128,1024]{2,1,0:T(8,128)(2,1)S(1)} %all-to-all-done.q_ref) | copy-start | bytes 3145732
  60.1 1.0 %copy-start.2 = (bf16[16,264,128]{2,1,0:T(8,128)(2,1)}, bf16[16,264,128]{2,1,0:T(8,128)(2,1)S(1)}, u32[]{:S(2)}) copy-start(bf16[16,264,128]{2,1,0:T(8,128)(2,1)S(1)} %collective-permute-done.mate_ref) | copy-start | bytes 3244036

commit v2 on v0

v2 whole, which is shorter than its diff:
```python
import functools

import jax
import jax.numpy as jnp
from jax import lax
from jax.experimental import pallas as pl
from jax.experimental.pallas import tpu as pltpu
from jax.sharding import Mesh
from jax.sharding import PartitionSpec as P


HEAD_SIZE = 128
DOCUMENTS = 8
LOG2E = 1.4426950408889634
LOW = -1e30
AXES = ("outer", "group", "core", "uly")
VMEM = pl.BlockSpec(memory_space=pltpu.VMEM)
HBM = pl.BlockSpec(memory_space=pl.ANY)


def pack(q_ref, k_ref, v_ref, seg_ref, kv_ref, *rest, outer, groups, layers):
    q_out, sems = rest[:groups], rest[groups]
    rows, width = q_out[0].shape
    mine = lax.axis_index("group")
    copies = []
    for i in range(groups):
        start = pl.multiple_of((mine ^ i) * width, width)
        copies.append(pltpu.make_async_copy(q_ref.at[:, pl.ds(start, width)], q_out[i], sems.at[i]))
        copies[-1].start()
    number = lax.broadcasted_iota(jnp.int32, (DOCUMENTS, rows), 0)
    below = jnp.where(seg_ref[...] < number, 1.0, 0.0)
    counts = jnp.broadcast_to(jnp.sum(below, axis=1, keepdims=True), (DOCUMENTS, HEAD_SIZE)).astype(jnp.bfloat16)
    for g in range(groups):
        cut = slice(g * HEAD_SIZE, (g + 1) * HEAD_SIZE)
        k, v = k_ref[:, cut], v_ref[:, cut]
        for o in range(outer):
            for z in range(layers):
                to = (o * groups + g) * layers + z
                kv_ref[to, :rows, :] = k
                kv_ref[to, rows : 2 * rows, :] = v
                kv_ref[to, 2 * rows :, :] = counts
    for copy in copies:
        copy.wait()


def attend(q_ref, own_ref, mate_ref, out_ref, m_ref, l_ref, acc_ref, *, index, rows, groups, layers, split):
    width = q_ref.shape[1]
    per = width // HEAD_SIZE
    sources = own_ref.shape[0]
    block = layers * rows
    scale = HEAD_SIZE ** -0.5 * LOG2E
    core, layer = lax.axis_index("core"), lax.axis_index("uly")
    home = lax.axis_index("outer") * groups + (lax.axis_index("group") ^ index)

    ends = jnp.zeros((DOCUMENTS, HEAD_SIZE), jnp.float32)
    for ref in (own_ref, mate_ref):
        for i in range(sources):
            ends = ends + ref[i, 2 * rows :, :].astype(jnp.float32)
    blk = home * 2 + core
    first = (blk * layers + layer) * rows
    place = first + lax.broadcasted_iota(jnp.int32, (rows, HEAD_SIZE), 0)
    start = jnp.zeros((rows, HEAD_SIZE), jnp.int32)
    for d in range(DOCUMENTS):
        end = jnp.broadcast_to(ends[d : d + 1], (rows, HEAD_SIZE)).astype(jnp.int32)
        start = jnp.where(end <= place, jnp.maximum(start, end), start)
    place, start = place[:, :1], start[:, :1]
    low_blk = jnp.min(start) // block
    m_ref[...] = jnp.full(m_ref.shape, LOW, jnp.float32)
    l_ref[...] = jnp.zeros(l_ref.shape, jnp.float32)
    acc_ref[...] = jnp.zeros(acc_ref.shape, jnp.float32)
    part = per // split

    def step(ref, chip, parity):
        base = (chip * 2 + parity) * block
        k = jnp.concatenate([ref[chip * layers + z, :rows, :] for z in range(layers)], axis=0)
        v = jnp.concatenate([ref[chip * layers + z, rows : 2 * rows, :] for z in range(layers)], axis=0)
        key = base + lax.broadcasted_iota(jnp.int32, (rows, block), 1)
        bias = jnp.where((key <= place) & (key >= start), 0.0, LOW)
        for h0 in range(0, per, part):
            q = jnp.concatenate([q_ref[:, h * HEAD_SIZE : (h + 1) * HEAD_SIZE] for h in range(h0, h0 + part)], axis=0)
            s = lax.dot_general(q, k, (((1,), (1,)), ((), ())), preferred_element_type=jnp.float32)
            ps = []
            factors = []
            for i in range(part):
                r = pl.ds((h0 + i) * rows, rows)
                x = s[i * rows : (i + 1) * rows] * scale + bias
                old = m_ref[r, :]
                top = jnp.maximum(old, jnp.max(x, axis=1, keepdims=True))
                p = jnp.exp2(x - top[:, :1])
                factor = jnp.exp2(old - top)
                m_ref[r, :] = top
                l_ref[r, :] = l_ref[r, :] * factor + jnp.sum(p, axis=1, keepdims=True)
                ps.append(p.astype(jnp.bfloat16))
                factors.append(factor)
            pv = lax.dot_general(
                jnp.concatenate(ps, axis=0), v, (((1,), (0,)), ((), ())), preferred_element_type=jnp.float32
            )
            r = pl.ds(h0 * rows, part * rows)
            acc_ref[r, :] = acc_ref[r, :] * jnp.concatenate(factors, axis=0) + pv

    @pl.loop((low_blk - core + 1) // 2, home + 1)
    def _(chip):
        step(own_ref, chip, core)

    other = 1 - core

    @pl.loop((low_blk - other + 1) // 2, home + core)
    def _(chip):
        step(mate_ref, chip, other)

    for h in range(per):
        r = pl.ds(h * rows, rows)
        out_ref[:, h * HEAD_SIZE : (h + 1) * HEAD_SIZE] = (acc_ref[r, :] / l_ref[r, :]).astype(out_ref.dtype)


def place(*refs, groups):
    pieces, out_ref, sems = refs[:groups], refs[groups], refs[groups + 1]
    width = pieces[0].shape[1]
    mine = lax.axis_index("group")
    copies = []
    for i in range(groups):
        start = pl.multiple_of((mine ^ i) * width, width)
        copies.append(pltpu.make_async_copy(pieces[i], out_ref.at[:, pl.ds(start, width)], sems.at[i]))
        copies[-1].start()
    for copy in copies:
        copy.wait()


def local(queries, keys, values, segments, *, outer, groups, layers):
    rows = queries.shape[0]
    width = queries.shape[1] // groups
    per = width // HEAD_SIZE
    members = outer * groups * layers
    sizes = dict(groups=groups, layers=layers)
    piece = jax.ShapeDtypeStruct((rows, width), jnp.bfloat16)
    kv, *q = pl.pallas_call(
        functools.partial(pack, outer=outer, **sizes),
        out_shape=[jax.ShapeDtypeStruct((members, 2 * rows + DOCUMENTS, HEAD_SIZE), jnp.bfloat16)] + [piece] * groups,
        in_specs=[HBM, VMEM, VMEM, VMEM],
        out_specs=[VMEM] * (groups + 1),
        scratch_shapes=[pltpu.SemaphoreType.DMA((groups,))],
        compiler_params=pltpu.CompilerParams(vmem_limit_bytes=16 << 20),
        name="pack",
    )(queries, keys, values, segments.reshape(1, rows))
    own = lax.all_to_all(kv, ("outer", "group", "uly"), split_axis=0, concat_axis=0, tiled=True)

    def swap(x, i):
        return lax.ppermute(x, "group", [(g, g ^ i) for g in range(groups)])

    order = list(range(groups - 1, 0, -1))
    for i in order:
        q[i] = swap(q[i], i)
    own, *q[1:] = lax.optimization_barrier((own, *q[1:]))
    mate = lax.ppermute(own, "core", [(0, 1), (1, 0)])
    out = [None] * groups
    before = None
    for i in order + [0]:
        if before is not None:
            q[i], before = lax.optimization_barrier((q[i], before))
        call = pl.pallas_call(
            functools.partial(attend, index=i, rows=rows, split=2, **sizes),
            out_shape=piece,
            in_specs=[VMEM] * 3,
            out_specs=VMEM,
            scratch_shapes=[pltpu.VMEM((per * rows, HEAD_SIZE), jnp.float32)] * 3,
            compiler_params=pltpu.CompilerParams(vmem_limit_bytes=24 << 20),
            cost_estimate=pl.CostEstimate(
                flops=2 * rows * width * members * rows, transcendentals=0, bytes_accessed=4 * rows * width
            ),
            name="attend",
        )
        before = out[i] = call(q[i], own, mate)
        if i:
            out[i] = swap(out[i], i)
    return pl.pallas_call(
        functools.partial(place, groups=groups),
        out_shape=jax.ShapeDtypeStruct(queries.shape, jnp.bfloat16),
        in_specs=[VMEM] * groups,
        out_specs=HBM,
        scratch_shapes=[pltpu.SemaphoreType.DMA((groups,))],
        compiler_params=pltpu.CompilerParams(vmem_limit_bytes=8 << 20),
        name="place",
    )(*out)


def solution(mesh):
    blocks, layers = mesh.shape["blk"], mesh.shape["uly"]

    def run(queries, keys, values, segments):
        groups = keys.shape[1] // HEAD_SIZE
        outer = blocks // 2 // groups
        fine = Mesh(mesh.devices.reshape(outer, groups, 2, layers), AXES)

        def body(*args):
            return local(*args, outer=outer, groups=groups, layers=layers)

        spec = P(AXES)
        step = jax.shard_map(body, mesh=fine, in_specs=(spec,) * 4, out_specs=spec, check_vma=False)
        return step(queries, keys, values, segments)

    return run
```

time: 266 us -> 72.9 us (0.27)
  the two profiles are of different devices: /device:TPU:7 before, /device:TPU:0 now
where the time goes in v2:
time: 72.9 us; the launch traced here: 72.6 us
  waiting for transfers between devices  33.3 us (46%)
  Pallas kernels  20.1 us (28%)
  starting transfers between devices  15.4 us (21%)
  local copies, waits for them, and re-layouts  3.69 us (5%)
    ppermute x6, waiting for transfers between devices, swap(): return lax.ppermute(x, 'group', [(g, g ^ i) for g in range(groups)])  26.9 us
    pallas_call x4, Pallas kernels, local(): before = out[i] = call(q[i], own, mate)  17.9 us
    all_to_all x1, starting transfers between devices, local(): lax.all_to_all(kv, ('outer', 'group', 'uly'), split_axis=0, concat_axis=0...  8.35 us
    ppermute x6, starting transfers between devices, swap(): return lax.ppermute(x, 'group', [(g, g ^ i) for g in range(groups)])  7.09 us
    unnamed x8, local copies, waits for them, and re-layouts  3.69 us
    all_to_all x1, waiting for transfers between devices, local(): lax.all_to_all(kv, ('outer', 'group', 'uly'), split_axis=0, concat_axis=0...  3.64 us
    ppermute x1, waiting for transfers between devices, local(): mate = lax.ppermute(own, 'core', [(0, 1), (1, 0)])  2.7 us
  transfers between devices with their start and end apart: 8, of which 6 were waited for; matrix products, arithmetic and copies ran while one was open for 0% of the time, Pallas kernels for 3%

profile of v2, /device:TPU:0, one launch (start us, length us, event | category | flops | bytes accessed | tf_op | source)
XLA Modules:
  0.0 72.6 jit_solution(1611790729450119818)
XLA Ops:
  0.0 1.2 %copy-done = bf16[128,4096]{1,0:T(8,128)(2,1)S(1)} copy-done((bf16[128,4096]{1,0:T(8,128)(2,1)S(1)}, bf16[128,4096]{1,0:T(8,128)(2,1)}, u32[]{:S(2)}) %copy-start) | copy-done | bytes 1048600
  1.2 0.9 %copy-done.1 = bf16[128,512]{1,0:T(8,128)(2,1)S(1)} copy-done((bf16[128,512]{1,0:T(8,128)(2,1)S(1)}, bf16[128,512]{1,0:T(8,128)(2,1)}, u32[]{:S(2)}) %copy-start.1) | copy-done | bytes 131096
  2.1 0.9 %copy-done.2 = bf16[128,512]{1,0:T(8,128)(2,1)S(1)} copy-done((bf16[128,512]{1,0:T(8,128)(2,1)S(1)}, bf16[128,512]{1,0:T(8,128)(2,1)}, u32[]{:S(2)}) %copy-start.2) | copy-done | bytes 131096
  3.0 0.7 copy-done.3
  3.7 1.2 %pack.1 = (bf16[16,264,128]{2,1,0:T(8,128)(2,1)}, bf16[128,1024]{1,0:T(8,128)(2,1)S(1)}, bf16[128,1024]{1,0:T(8,128)(2,1)S(1)}, bf16[128,1024]{1,0:T(8,128)(2,1)S(1)}, bf16[128,1024]{1,0:T(8,128)(2,1)S(1)}) custom-call(bf16[128,4096]{1,0:T(8,128)(2,1)S(1)} %copy-done, bf16[128,512]{1,0:T(8,128)(2,1)S(1)} %copy-done.1, bf16[128,512]{1,0:T(8,128)(2,1)S(1)} %copy-done.2, ...), custom_call_target="tpu_custom_call" | custom-call | tf_op jit(solution)/shard_map/pack/pallas_call | solution.py:136
  4.9 8.4 %all-to-all-start = ((bf16[16,264,128]{2,1,0:T(8,128)(2,1)}), bf16[16,264,128]{2,1,0:T(8,128)(2,1)S(1)}, u32[]{:S(2)}, u32[]{:S(2)}) async-start(bf16[16,264,128]{2,1,0:T(8,128)(2,1)} %get-tuple-element.18), calls=%async_computation | async-start | bytes 2162688 | tf_op jit(solution)/shard_map/all_to_all | solution.py:145
  13.3 1.9 %collective-permute-start = (bf16[128,1024]{1,0:T(8,128)(2,1)S(1)}, bf16[128,1024]{1,0:T(8,128)(2,1)S(1)}, u32[]{:S(2)}, u32[]{:S(2)}) collective-permute-start(bf16[128,1024]{1,0:T(8,128)(2,1)S(1)} %get-tuple-element.19), channel_id=1, source_target_pairs={{0,8},{8,0},{16,24},{24,16},{1,9},{9,1},{17,25},{25,17},{2,10},{10... | collective-permute-start | bytes 786440 | tf_op jit(solution)/shard_map/ppermute | solution.py:148
  15.2 1.5 %collective-permute-start.1 = (bf16[128,1024]{1,0:T(8,128)(2,1)S(1)}, bf16[128,1024]{1,0:T(8,128)(2,1)S(1)}, u32[]{:S(2)}, u32[]{:S(2)}) collective-permute-start(bf16[128,1024]{1,0:T(8,128)(2,1)S(1)} %get-tuple-element.20), channel_id=1, source_target_pairs={{0,16},{8,24},{16,0},{24,8},{1,17},{9,25},{17,1},{25,9},{2,18},{10... | collective-permute-start | bytes 786440 | tf_op jit(solution)/shard_map/ppermute | solution.py:148
  16.7 0.2 collective-permute-start.2
  16.9 15.5 %collective-permute-done.q_ref = bf16[128,1024]{1,0:T(8,128)(2,1)S(1)} collective-permute-done((bf16[128,1024]{1,0:T(8,128)(2,1)S(1)}, bf16[128,1024]{1,0:T(8,128)(2,1)S(1)}, u32[]{:S(2)}, u32[]{:S(2)}) %collective-permute-start) | collective-permute-done | bytes 262176 | tf_op jit(solution)/shard_map/ppermute | solution.py:148
  32.3 0.0 collective-permute-done.1.q_ref
  32.3 5.5 %collective-permute-done.2.q_ref = bf16[128,1024]{1,0:T(8,128)(2,1)S(1)} collective-permute-done((bf16[128,1024]{1,0:T(8,128)(2,1)S(1)}, bf16[128,1024]{1,0:T(8,128)(2,1)S(1)}, u32[]{:S(2)}, u32[]{:S(2)}) %collective-permute-start.2) | collective-permute-done | bytes 262176 | tf_op jit(solution)/shard_map/ppermute | solution.py:148
  37.8 3.6 %all-to-all-done.own_ref = bf16[16,264,128]{2,1,0:T(8,128)(2,1)S(1)} async-done(((bf16[16,264,128]{2,1,0:T(8,128)(2,1)}), bf16[16,264,128]{2,1,0:T(8,128)(2,1)S(1)}, u32[]{:S(2)}, u32[]{:S(2)}) %all-to-all-start) | async-done | bytes 1081376 | tf_op jit(solution)/shard_map/all_to_all | solution.py:145
  41.5 2.7 %collective-permute-done.3.mate_ref = bf16[16,264,128]{2,1,0:T(8,128)(2,1)S(1)} collective-permute-done((bf16[16,264,128]{2,1,0:T(8,128)(2,1)S(1)}, bf16[16,264,128]{2,1,0:T(8,128)(2,1)S(1)}, u32[]{:S(2)}, u32[]{:S(2)}) %collective-permute-start.3) | collective-permute-done | bytes 1081376 | tf_op jit(solution)/shard_map/ppermute | solution.py:154
  44.2 7.8 %attend.4 = bf16[128,1024]{1,0:T(8,128)(2,1)S(1)} custom-call(bf16[128,1024]{1,0:T(8,128)(2,1)S(1)} %collective-permute-done.2.q_ref, bf16[16,264,128]{2,1,0:T(8,128)(2,1)S(1)} %all-to-all-done.own_ref, bf16[16,264,128]{2,1,0:T(8,128)(2,1)S(1)} %collective-permute-done.3.mate_ref), custom_call_target="tpu_custom_call" | custom-call | flops 536870912 | bytes 524288 | tf_op jit(solution)/shard_map/attend/pallas_call | solution.py:172
  52.0 4.8 %attend.5 = bf16[128,1024]{1,0:T(8,128)(2,1)S(1)} custom-call(bf16[128,1024]{1,0:T(8,128)(2,1)S(1)} %collective-permute-done.1.q_ref, bf16[16,264,128]{2,1,0:T(8,128)(2,1)S(1)} %all-to-all-done.own_ref, bf16[16,264,128]{2,1,0:T(8,128)(2,1)S(1)} %collective-permute-done.3.mate_ref), custom_call_target="tpu_custom_call" | custom-call | flops 536870912 | bytes 524288 | tf_op jit(solution)/shard_map/attend/pallas_call | solution.py:172
  56.9 3.4 %attend.6 = bf16[128,1024]{1,0:T(8,128)(2,1)S(1)} custom-call(bf16[128,1024]{1,0:T(8,128)(2,1)S(1)} %collective-permute-done.q_ref, bf16[16,264,128]{2,1,0:T(8,128)(2,1)S(1)} %all-to-all-done.own_ref, bf16[16,264,128]{2,1,0:T(8,128)(2,1)S(1)} %collective-permute-done.3.mate_ref), custom_call_target="tpu_custom_call" | custom-call | flops 536870912 | bytes 524288 | tf_op jit(solution)/shard_map/attend/pallas_call | solution.py:172
  60.2 0.1 collective-permute-start.4
  60.3 0.1 collective-permute-start.5
  60.4 3.4 %collective-permute-start.6 = (bf16[128,1024]{1,0:T(8,128)(2,1)S(1)}, bf16[128,1024]{1,0:T(8,128)(2,1)S(1)}, u32[]{:S(2)}, u32[]{:S(2)}) collective-permute-start(bf16[128,1024]{1,0:T(8,128)(2,1)S(1)} %attend.4), channel_id=1, source_target_pairs={{0,24},{8,16},{16,8},{24,0},{1,25},{9,17},{17,9},{25,1},{2,26},{10... | collective-permute-start | bytes 786440 | tf_op jit(solution)/shard_map/ppermute | solution.py:148
  63.8 1.9 %attend.7.refs_0_ = bf16[128,1024]{1,0:T(8,128)(2,1)S(1)} custom-call(bf16[128,1024]{1,0:T(8,128)(2,1)S(1)} %get-tuple-element.28.q_ref, bf16[16,264,128]{2,1,0:T(8,128)(2,1)S(1)} %all-to-all-done.own_ref, bf16[16,264,128]{2,1,0:T(8,128)(2,1)S(1)} %collective-permute-done.3.mate_ref), custom_call_target="tpu_custom_call" | custom-call | flops 536870912 | bytes 524288 | tf_op jit(solution)/shard_map/attend/pallas_call | solution.py:172
  65.7 2.9 %collective-permute-done.4.refs_1_ = bf16[128,1024]{1,0:T(8,128)(2,1)S(1)} collective-permute-done((bf16[128,1024]{1,0:T(8,128)(2,1)S(1)}, bf16[128,1024]{1,0:T(8,128)(2,1)S(1)}, u32[]{:S(2)}, u32[]{:S(2)}) %collective-permute-start.4) | collective-permute-done | bytes 262176 | tf_op jit(solution)/shard_map/ppermute | solution.py:148
  68.5 3.1 %collective-permute-done.5.refs_2_ = bf16[128,1024]{1,0:T(8,128)(2,1)S(1)} collective-permute-done((bf16[128,1024]{1,0:T(8,128)(2,1)S(1)}, bf16[128,1024]{1,0:T(8,128)(2,1)S(1)}, u32[]{:S(2)}, u32[]{:S(2)}) %collective-permute-start.5) | collective-permute-done | bytes 262176 | tf_op jit(solution)/shard_map/ppermute | solution.py:148
  71.6 1.0 %place.1 = bf16[128,4096]{1,0:T(8,128)(2,1)} custom-call(bf16[128,1024]{1,0:T(8,128)(2,1)S(1)} %attend.7.refs_0_, bf16[128,1024]{1,0:T(8,128)(2,1)S(1)} %collective-permute-done.4.refs_1_, bf16[128,1024]{1,0:T(8,128)(2,1)S(1)} %collective-permute-done.5.refs_2_, bf16[128,1024]{1,0:T(8,128)(2,1)S(1)} %collective-permute-done.6.refs_3_), custom_call_target="tpu_custom_call" | custom-call | tf_op jit(solution)/shard_map/place/pallas_call | solution.py:175
  (6 shorter events, 0.0 us)
Async XLA Ops:
  0.0 1.2 %copy-start = (bf16[128,4096]{1,0:T(8,128)(2,1)S(1)}, bf16[128,4096]{1,0:T(8,128)(2,1)}, u32[]{:S(2)}) copy-start(bf16[128,4096]{1,0:T(8,128)(2,1)} %q_ref.1) | copy-start | bytes 3145732
  1.2 0.9 %copy-start.1 = (bf16[128,512]{1,0:T(8,128)(2,1)S(1)}, bf16[128,512]{1,0:T(8,128)(2,1)}, u32[]{:S(2)}) copy-start(bf16[128,512]{1,0:T(8,128)(2,1)} %k_ref.1) | copy-start | bytes 393220
  2.1 0.9 %copy-start.2 = (bf16[128,512]{1,0:T(8,128)(2,1)S(1)}, bf16[128,512]{1,0:T(8,128)(2,1)}, u32[]{:S(2)}) copy-start(bf16[128,512]{1,0:T(8,128)(2,1)} %v_ref.1) | copy-start | bytes 393220
  3.0 0.7 copy-start.3
  4.9 36.5 %all-to-all-start = ((bf16[16,264,128]{2,1,0:T(8,128)(2,1)}), bf16[16,264,128]{2,1,0:T(8,128)(2,1)S(1)}, u32[]{:S(2)}, u32[]{:S(2)}) async-start(bf16[16,264,128]{2,1,0:T(8,128)(2,1)} %get-tuple-element.18), calls=%async_computation | async-start | bytes 2162688 | tf_op jit(solution)/shard_map/all_to_all | solution.py:145
  13.3 19.0 %collective-permute-start = (bf16[128,1024]{1,0:T(8,128)(2,1)S(1)}, bf16[128,1024]{1,0:T(8,128)(2,1)S(1)}, u32[]{:S(2)}, u32[]{:S(2)}) collective-permute-start(bf16[128,1024]{1,0:T(8,128)(2,1)S(1)} %get-tuple-element.19), channel_id=1, source_target_pairs={{0,8},{8,0},{16,24},{24,16},{1,9},{9,1},{17,25},{25,17},{2,10},{10... | collective-permute-start | bytes 786440 | tf_op jit(solution)/shard_map/ppermute | solution.py:148
  15.2 17.1 %collective-permute-start.1 = (bf16[128,1024]{1,0:T(8,128)(2,1)S(1)}, bf16[128,1024]{1,0:T(8,128)(2,1)S(1)}, u32[]{:S(2)}, u32[]{:S(2)}) collective-permute-start(bf16[128,1024]{1,0:T(8,128)(2,1)S(1)} %get-tuple-element.20), channel_id=1, source_target_pairs={{0,16},{8,24},{16,0},{24,8},{1,17},{9,25},{17,1},{25,9},{2,18},{10... | collective-permute-start | bytes 786440 | tf_op jit(solution)/shard_map/ppermute | solution.py:148
  16.7 21.1 %collective-permute-start.2 = (bf16[128,1024]{1,0:T(8,128)(2,1)S(1)}, bf16[128,1024]{1,0:T(8,128)(2,1)S(1)}, u32[]{:S(2)}, u32[]{:S(2)}) collective-permute-start(bf16[128,1024]{1,0:T(8,128)(2,1)S(1)} %get-tuple-element.21), channel_id=1, source_target_pairs={{0,24},{8,16},{16,8},{24,0},{1,25},{9,17},{17,9},{25,1},{2,26},{10... | collective-permute-start | bytes 786440 | tf_op jit(solution)/shard_map/ppermute | solution.py:148
  41.5 2.7 %collective-permute-start.3 = (bf16[16,264,128]{2,1,0:T(8,128)(2,1)S(1)}, bf16[16,264,128]{2,1,0:T(8,128)(2,1)S(1)}, u32[]{:S(2)}, u32[]{:S(2)}) collective-permute-start(bf16[16,264,128]{2,1,0:T(8,128)(2,1)S(1)} %all-to-all-done.own_ref), channel_id=1, source_target_pairs={{0,4},{4,0},{1,5},{5,1},{2,6},{6,2},{3,7},{7,3},{8,12},{12,8},{9,1... | collective-permute-start | bytes 3244040 | tf_op jit(solution)/shard_map/ppermute | solution.py:154
  60.2 8.3 %collective-permute-start.4 = (bf16[128,1024]{1,0:T(8,128)(2,1)S(1)}, bf16[128,1024]{1,0:T(8,128)(2,1)S(1)}, u32[]{:S(2)}, u32[]{:S(2)}) collective-permute-start(bf16[128,1024]{1,0:T(8,128)(2,1)S(1)} %attend.6), channel_id=1, source_target_pairs={{0,8},{8,0},{16,24},{24,16},{1,9},{9,1},{17,25},{25,17},{2,10},{10... | collective-permute-start | bytes 786440 | tf_op jit(solution)/shard_map/ppermute | solution.py:148
  60.3 11.3 %collective-permute-start.5 = (bf16[128,1024]{1,0:T(8,128)(2,1)S(1)}, bf16[128,1024]{1,0:T(8,128)(2,1)S(1)}, u32[]{:S(2)}, u32[]{:S(2)}) collective-permute-start(bf16[128,1024]{1,0:T(8,128)(2,1)S(1)} %attend.5), channel_id=1, source_target_pairs={{0,16},{8,24},{16,0},{24,8},{1,17},{9,25},{17,1},{25,9},{2,18},{10... | collective-permute-start | bytes 786440 | tf_op jit(solution)/shard_map/ppermute | solution.py:148
  60.4 11.3 %collective-permute-start.6 = (bf16[128,1024]{1,0:T(8,128)(2,1)S(1)}, bf16[128,1024]{1,0:T(8,128)(2,1)S(1)}, u32[]{:S(2)}, u32[]{:S(2)}) collective-permute-start(bf16[128,1024]{1,0:T(8,128)(2,1)S(1)} %attend.4), channel_id=1, source_target_pairs={{0,24},{8,16},{16,8},{24,0},{1,25},{9,17},{17,9},{25,1},{2,26},{10... | collective-permute-start | bytes 786440 | tf_op jit(solution)/shard_map/ppermute | solution.py:148

commit v3 on v2

v3 whole, which is shorter than its diff:
```python
import functools

import jax
import jax.numpy as jnp
from jax import lax
from jax.experimental import pallas as pl
from jax.experimental.pallas import tpu as pltpu
from jax.sharding import Mesh
from jax.sharding import PartitionSpec as P


HEAD_SIZE = 128
DOCUMENTS = 8
LOG2E = 1.4426950408889634
LOW = -1e30
AXES = ("outer", "group", "core", "uly")
VMEM = pl.BlockSpec(memory_space=pltpu.VMEM)
HBM = pl.BlockSpec(memory_space=pltpu.HBM)


def pack(q_ref, k_ref, v_ref, seg_ref, *rest, groups):
    kv_out, q_out, (k_buf, v_buf, seg_buf, sems) = rest[:groups], rest[groups : 2 * groups], rest[2 * groups :]
    rows, width = q_out[0].shape
    mine = lax.axis_index("group")
    first = [
        pltpu.make_async_copy(seg_ref, seg_buf, sems.at[groups]),
        pltpu.make_async_copy(k_ref, k_buf, sems.at[groups + 1]),
        pltpu.make_async_copy(v_ref, v_buf, sems.at[groups + 2]),
    ]
    later = []
    for i in range(groups):
        start = pl.multiple_of((mine ^ i) * width, width)
        later.append(pltpu.make_async_copy(q_ref.at[:, pl.ds(start, width)], q_out[i], sems.at[i]))
    for copy in first + later:
        copy.start()
    first[0].wait()
    number = lax.broadcasted_iota(jnp.int32, (DOCUMENTS, rows), 0)
    below = jnp.where(seg_buf[...] < number, 1.0, 0.0)
    counts = jnp.broadcast_to(jnp.sum(below, axis=1, keepdims=True), (DOCUMENTS, HEAD_SIZE)).astype(jnp.bfloat16)
    first[1].wait()
    first[2].wait()
    for i in range(groups):
        cut = pl.ds(pl.multiple_of((mine ^ i) * HEAD_SIZE, HEAD_SIZE), HEAD_SIZE)
        kv_out[i][:rows, :] = k_buf[:, cut]
        kv_out[i][rows : 2 * rows, :] = v_buf[:, cut]
        kv_out[i][2 * rows :, :] = counts
    for copy in later:
        copy.wait()


def merge(*refs, groups):
    pieces, out_ref = refs[:groups], refs[groups]
    mine = lax.axis_index("group")
    for i in range(groups):
        out_ref[mine ^ i] = pieces[i][...]


def attend(*refs, index, turns, rows, groups, layers, split, final):
    count = len(turns)
    q_ref, home_ref = refs[:2]
    own, mate = refs[2 : 2 + count], refs[2 + count : 2 + 2 * count]
    rest = refs[2 + 2 * count :]
    if final:
        state, out_ref, held = rest[:3], rest[3], rest[4:]
    else:
        held = rest
    m_ref, l_ref, acc_ref = held
    per = q_ref.shape[1] // HEAD_SIZE
    chips = own[0].shape[0]
    scale = HEAD_SIZE ** -0.5 * LOG2E
    core, layer = lax.axis_index("core"), lax.axis_index("uly")
    home = lax.axis_index("outer") * groups + (lax.axis_index("group") ^ index)
    shape = (rows, HEAD_SIZE)
    lane = lax.broadcasted_iota(jnp.int32, (DOCUMENTS, HEAD_SIZE), 1).astype(jnp.float32)
    number = lax.broadcasted_iota(jnp.int32, (DOCUMENTS, HEAD_SIZE), 0).astype(jnp.float32)

    def counts(ref, chip):
        return ref[chip, 2 * rows :, :].astype(jnp.float32)

    mine = counts(home_ref, home)
    local_row = lax.broadcasted_iota(jnp.int32, shape, 0).astype(jnp.float32)
    row_doc = jnp.zeros(shape, jnp.float32)
    for d in range(DOCUMENTS):
        row_doc = row_doc + jnp.where(jnp.broadcast_to(mine[d : d + 1], shape) <= local_row, 1.0, 0.0)
    place = ((home * 2 + core) * layers + layer) * rows + lax.broadcasted_iota(jnp.int32, shape, 0)
    earliest = row_doc[:1] - 1.0

    def skipped(tiles):
        gone = jnp.zeros((1, HEAD_SIZE), jnp.float32)
        for chip in range(chips):
            least = None
            for ref in tiles:
                held_below = jnp.sum(jnp.where(number == earliest, counts(ref, chip), 0.0), axis=0, keepdims=True)
                least = held_below if least is None else jnp.minimum(least, held_below)
            gone = gone + jnp.where(least >= rows, 1.0, 0.0)
        return jnp.max(gone).astype(jnp.int32)

    if final:
        for into, ref in zip(held, state):
            into[...] = ref[...]
    else:
        m_ref[...] = jnp.full(m_ref.shape, LOW, jnp.float32)
        l_ref[...] = jnp.zeros(l_ref.shape, jnp.float32)
        acc_ref[...] = jnp.zeros(acc_ref.shape, jnp.float32)
    part = per // split

    def step(tiles, chip, parity):
        k = jnp.concatenate([ref[chip, :rows, :] for ref in tiles], axis=0)
        v = jnp.concatenate([ref[chip, rows : 2 * rows, :] for ref in tiles], axis=0)
        bias = []
        for turn, ref in zip(turns, tiles):
            base = ((chip * 2 + parity) * layers + (layer ^ turn)) * rows
            key_doc = jnp.sum(jnp.where(counts(ref, chip) <= lane, 1.0, 0.0), axis=0, keepdims=True)
            key = base + lax.broadcasted_iota(jnp.int32, shape, 1)
            bias.append(jnp.where((key <= place) & (row_doc == key_doc), 0.0, LOW))
        for h0 in range(0, per, part):
            q = jnp.concatenate([q_ref[:, h * HEAD_SIZE : (h + 1) * HEAD_SIZE] for h in range(h0, h0 + part)], axis=0)
            s = lax.dot_general(q, k, (((1,), (1,)), ((), ())), preferred_element_type=jnp.float32)
            ps = []
            factors = []
            for i in range(part):
                r = pl.ds((h0 + i) * rows, rows)
                xs = [s[i * rows : (i + 1) * rows, c * rows : (c + 1) * rows] + bias[c] for c in range(count)]
                old = m_ref[r, :]
                top = jnp.maximum(old, jnp.max(functools.reduce(jnp.maximum, xs), axis=1, keepdims=True))
                m_ref[r, :] = top
                shift = top * scale
                p = [jnp.exp2(x * scale - shift) for x in xs]
                factor = jnp.exp2(old * scale - shift)
                l_ref[r, :] = l_ref[r, :] * factor + functools.reduce(jnp.add, p)
                ps.append(jnp.concatenate([y.astype(jnp.bfloat16) for y in p], axis=1))
                factors.append(factor)
            pv = lax.dot_general(
                jnp.concatenate(ps, axis=0), v, (((1,), (0,)), ((), ())), preferred_element_type=jnp.float32
            )
            r = pl.ds(h0 * rows, part * rows)
            acc_ref[r, :] = acc_ref[r, :] * jnp.concatenate(factors, axis=0) + pv

    @pl.loop(skipped(own), home + 1)
    def _(chip):
        step(own, chip, core)

    @pl.loop(skipped(mate), home + core)
    def _(chip):
        step(mate, chip, 1 - core)

    if final:
        for h in range(per):
            r = pl.ds(h * rows, rows)
            total = jnp.sum(l_ref[r, :], axis=1, keepdims=True)
            out_ref[:, h * HEAD_SIZE : (h + 1) * HEAD_SIZE] = (acc_ref[r, :] / total).astype(out_ref.dtype)


def place(*refs, groups):
    pieces, out_ref, sems = refs[:groups], refs[groups], refs[groups + 1]
    width = pieces[0].shape[1]
    mine = lax.axis_index("group")
    copies = []
    for i in range(groups):
        start = pl.multiple_of((mine ^ i) * width, width)
        copies.append(pltpu.make_async_copy(pieces[i], out_ref.at[:, pl.ds(start, width)], sems.at[i]))
        copies[-1].start()
    for copy in copies:
        copy.wait()


def limit(mib):
    return pltpu.CompilerParams(vmem_limit_bytes=mib << 20)


def local(queries, keys, values, segments, *, outer, groups, layers):
    rows = queries.shape[0]
    width = queries.shape[1] // groups
    per = width // HEAD_SIZE
    piece = jax.ShapeDtypeStruct((rows, width), jnp.bfloat16)
    one = jax.ShapeDtypeStruct((2 * rows + DOCUMENTS, HEAD_SIZE), jnp.bfloat16)
    made = pl.pallas_call(
        functools.partial(pack, groups=groups),
        out_shape=[one] * groups + [piece] * groups,
        in_specs=[HBM] * 4,
        out_specs=[VMEM] * (2 * groups),
        scratch_shapes=[
            pltpu.VMEM(keys.shape, jnp.bfloat16),
            pltpu.VMEM(values.shape, jnp.bfloat16),
            pltpu.VMEM((1, rows), jnp.int32),
            pltpu.SemaphoreType.DMA((groups + 3,)),
        ],
        compiler_params=limit(8),
        name="pack",
    )(*(pltpu.with_memory_space_constraint(x, pltpu.HBM) for x in (queries, keys, values, segments.reshape(1, rows))))
    kv, q = list(made[:groups]), list(made[groups:])

    def swap(x, axis, size, i):
        return lax.ppermute(x, axis, [(g, g ^ i) for g in range(size)])

    order = list(range(groups - 1, 0, -1))
    for i in order:
        kv[i] = swap(kv[i], "group", groups, i)
    for i in order:
        q[i] = swap(q[i], "group", groups, i)
    mine = pl.pallas_call(
        functools.partial(merge, groups=groups),
        out_shape=jax.ShapeDtypeStruct((groups, *one.shape), jnp.bfloat16),
        in_specs=[VMEM] * groups,
        out_specs=VMEM,
        compiler_params=limit(4),
        name="merge",
    )(*kv)
    if outer > 1:
        mine = lax.all_gather(mine, "outer", axis=0, tiled=True)
    own = [mine] + [swap(mine, "uly", layers, j) for j in range(1, layers)]
    mate = []
    for j in range(layers):
        mate.append(lax.ppermute(own[j], "core", [(0, 1), (1, 0)]))

    held = [jax.ShapeDtypeStruct((per * rows, HEAD_SIZE), jnp.float32)] * 3
    common = dict(rows=rows, groups=groups, layers=layers, split=2)
    near, far = list(range(layers // 2)), list(range(layers // 2, layers))

    def call(i, turns, final, *args):
        return pl.pallas_call(
            functools.partial(attend, index=i, turns=turns, final=final, **common),
            out_shape=piece if final else held,
            in_specs=[VMEM] * len(args),
            out_specs=VMEM if final else [VMEM] * 3,
            scratch_shapes=[pltpu.VMEM(x.shape, x.dtype) for x in held] if final else [],
            compiler_params=limit(16),
            name="attend",
        )(*args)

    states = [None] * groups
    last = None
    for i in order + [0]:
        if last is not None:
            q[i], last = lax.optimization_barrier((q[i], last))
        states[i] = call(i, near, False, q[i], own[0], *(own[j] for j in near), *(mate[j] for j in near))
        last = states[i][0]
    out = [None] * groups
    last = None
    for i in order + [0]:
        if last is not None:
            q[i], last = lax.optimization_barrier((q[i], last))
        last = call(i, far, True, q[i], own[0], *(own[j] for j in far), *(mate[j] for j in far), *states[i])
        out[i] = swap(last, "group", groups, i) if i else last
    return pl.pallas_call(
        functools.partial(place, groups=groups),
        out_shape=jax.ShapeDtypeStruct(queries.shape, jnp.bfloat16),
        in_specs=[VMEM] * groups,
        out_specs=HBM,
        scratch_shapes=[pltpu.SemaphoreType.DMA((groups,))],
        compiler_params=limit(4),
        name="place",
    )(*out)


def solution(mesh):
    blocks, layers = mesh.shape["blk"], mesh.shape["uly"]

    def run(queries, keys, values, segments):
        groups = keys.shape[1] // HEAD_SIZE
        outer = blocks // 2 // groups
        fine = Mesh(mesh.devices.reshape(outer, groups, 2, layers), AXES)

        def body(*args):
            return local(*args, outer=outer, groups=groups, layers=layers)

        spec = P(AXES)
        step = jax.shard_map(body, mesh=fine, in_specs=(spec,) * 4, out_specs=spec, check_vma=False)
        return step(queries, keys, values, segments)

    return run
```

time: 72.9 us -> 72.3 us (level)
  the two profiles are of different devices: /device:TPU:0 before, /device:TPU:6 now
where the time goes in v3:
time: 72.3 us; the launch traced here: 72.2 us
  waiting for transfers between devices  27.6 us (38%)
  starting transfers between devices  23.3 us (32%)
  Pallas kernels  21.2 us (29%)
    ppermute x12, waiting for transfers between devices, swap(): return lax.ppermute(x, axis, [(g, g ^ i) for g in range(size)])  27.6 us
    ppermute x12, starting transfers between devices, swap(): return lax.ppermute(x, axis, [(g, g ^ i) for g in range(size)])  23.3 us
    pallas_call x8, Pallas kernels, call(): pl.pallas_call(functools.partial(attend, index=i, turns=turns, final=fina...  18.7 us
  transfers between devices with their start and end apart: 16, of which 6 were waited for; matrix products, arithmetic and copies ran while one was open for 0% of the time, Pallas kernels for 26%

profile of v3, /device:TPU:6, one launch (start us, length us, event | category | flops | bytes accessed | tf_op | source)
XLA Modules:
  0.0 72.2 jit_solution(1202343974951314815)
XLA Ops:
  0.0 1.4 %pack.1 = (bf16[264,128]{1,0:T(8,128)(2,1)S(1)}, bf16[264,128]{1,0:T(8,128)(2,1)S(1)}, bf16[264,128]{1,0:T(8,128)(2,1)S(1)}, bf16[264,128]{1,0:T(8,128)(2,1)S(1)...) custom-call(bf16[128,4096]{1,0:T(8,128)(2,1)} %q_ref.1, ...), custom_call_target="tpu_custom_call" | custom-call | tf_op jit(solution)/shard_map/pack/pallas_call | solution.py:177
  2.1 2.9 %collective-permute-start.5 = (bf16[264,128]{1,0:T(8,128)(2,1)S(1)}, bf16[264,128]{1,0:T(8,128)(2,1)S(1)}, u32[]{:S(2)}, u32[]{:S(2)}) collective-permute-start(bf16[264,128]{1,0:T(8,128)(2,1)S(1)} %get-tuple-element.38), channel_id=1, source_target_pairs={{0,24},{8,16},{16,8},{24,0},{1,25},{9,17},{17,9},{25,1},{2,26},{10... | collective-permute-start | bytes 202760 | tf_op jit(solution)/shard_map/ppermute | solution.py:194
  5.0 1.2 %collective-permute-done.3.refs_1_ = bf16[264,128]{1,0:T(8,128)(2,1)S(1)} collective-permute-done((bf16[264,128]{1,0:T(8,128)(2,1)S(1)}, bf16[264,128]{1,0:T(8,128)(2,1)S(1)}, u32[]{:S(2)}, u32[]{:S(2)}) %collective-permute-start.3) | collective-permute-done | bytes 67616 | tf_op jit(solution)/shard_map/ppermute | solution.py:194
  6.2 1.3 %collective-permute-done.4.refs_2_ = bf16[264,128]{1,0:T(8,128)(2,1)S(1)} collective-permute-done((bf16[264,128]{1,0:T(8,128)(2,1)S(1)}, bf16[264,128]{1,0:T(8,128)(2,1)S(1)}, u32[]{:S(2)}, u32[]{:S(2)}) %collective-permute-start.4) | collective-permute-done | bytes 67616 | tf_op jit(solution)/shard_map/ppermute | solution.py:194
  7.5 1.8 %collective-permute-start.6 = (bf16[4,264,128]{2,1,0:T(8,128)(2,1)S(1)}, bf16[4,264,128]{2,1,0:T(8,128)(2,1)S(1)}, u32[]{:S(2)}, u32[]{:S(2)}) collective-permute-start(bf16[4,264,128]{2,1,0:T(8,128)(2,1)S(1)} %merge.1.refs_1_.refs_2_), channel_id=1, source_target_pairs={{0,1},{1,0},{2,3},{3,2},{4,5},{5,4},{6,7},{7,6},{8,9},{9,8},{10,11... | collective-permute-start | bytes 811016 | tf_op jit(solution)/shard_map/ppermute | solution.py:194
  9.4 2.5 %collective-permute-start.10 = (bf16[4,264,128]{2,1,0:T(8,128)(2,1)S(1)}, bf16[4,264,128]{2,1,0:T(8,128)(2,1)S(1)}, u32[]{:S(2)}, u32[]{:S(2)}) collective-permute-start(bf16[4,264,128]{2,1,0:T(8,128)(2,1)S(1)} %merge.1.refs_1_.refs_2_), channel_id=1, source_target_pairs={{0,3},{1,2},{2,1},{3,0},{4,7},{5,6},{6,5},{7,4},{8,11},{9,10},{10,... | collective-permute-start | bytes 811016 | tf_op jit(solution)/shard_map/ppermute | solution.py:194
  12.0 2.4 %collective-permute-start.2 = (bf16[128,1024]{1,0:T(8,128)(2,1)S(1)}, bf16[128,1024]{1,0:T(8,128)(2,1)S(1)}, u32[]{:S(2)}, u32[]{:S(2)}) collective-permute-start(bf16[128,1024]{1,0:T(8,128)(2,1)S(1)} %get-tuple-element.34), channel_id=1, source_target_pairs={{0,24},{8,16},{16,8},{24,0},{1,25},{9,17},{17,9},{25,1},{2,26},{10... | collective-permute-start | bytes 786440 | tf_op jit(solution)/shard_map/ppermute | solution.py:194
  14.4 1.8 %collective-permute-done.6.refs_3_ = bf16[4,264,128]{2,1,0:T(8,128)(2,1)S(1)} collective-permute-done((bf16[4,264,128]{2,1,0:T(8,128)(2,1)S(1)}, bf16[4,264,128]{2,1,0:T(8,128)(2,1)S(1)}, u32[]{:S(2)}, u32[]{:S(2)}) %collective-permute-start.6) | collective-permute-done | bytes 270368 | tf_op jit(solution)/shard_map/ppermute | solution.py:194
  16.2 8.8 %collective-permute-done.10.refs_3_ = bf16[4,264,128]{2,1,0:T(8,128)(2,1)S(1)} collective-permute-done((bf16[4,264,128]{2,1,0:T(8,128)(2,1)S(1)}, bf16[4,264,128]{2,1,0:T(8,128)(2,1)S(1)}, u32[]{:S(2)}, u32[]{:S(2)}) %collective-permute-start.10) | collective-permute-done | bytes 270368 | tf_op jit(solution)/shard_map/ppermute | solution.py:194
  25.1 9.3 %collective-permute-done.9.refs_2_ = bf16[4,264,128]{2,1,0:T(8,128)(2,1)S(1)} collective-permute-done((bf16[4,264,128]{2,1,0:T(8,128)(2,1)S(1)}, bf16[4,264,128]{2,1,0:T(8,128)(2,1)S(1)}, u32[]{:S(2)}, u32[]{:S(2)}) %collective-permute-start.9) | collective-permute-done | bytes 270368 | tf_op jit(solution)/shard_map/ppermute | solution.py:194
  34.4 1.4 %collective-permute-start.1 = (bf16[128,1024]{1,0:T(8,128)(2,1)S(1)}, bf16[128,1024]{1,0:T(8,128)(2,1)S(1)}, u32[]{:S(2)}, u32[]{:S(2)}) collective-permute-start(bf16[128,1024]{1,0:T(8,128)(2,1)S(1)} %get-tuple-element.33), channel_id=1, source_target_pairs={{0,16},{8,24},{16,0},{24,8},{1,17},{9,25},{17,1},{25,9},{2,18},{10... | collective-permute-start | bytes 786440 | tf_op jit(solution)/shard_map/ppermute | solution.py:194
  35.8 1.1 %collective-permute-start = (bf16[128,1024]{1,0:T(8,128)(2,1)S(1)}, bf16[128,1024]{1,0:T(8,128)(2,1)S(1)}, u32[]{:S(2)}, u32[]{:S(2)}) collective-permute-start(bf16[128,1024]{1,0:T(8,128)(2,1)S(1)} %get-tuple-element.32), channel_id=1, source_target_pairs={{0,8},{8,0},{16,24},{24,16},{1,9},{9,1},{17,25},{25,17},{2,10},{10... | collective-permute-start | bytes 786440 | tf_op jit(solution)/shard_map/ppermute | solution.py:194
  36.9 1.1 %attend.8 = (f32[1024,128]{1,0:T(8,128)S(1)}, f32[1024,128]{1,0:T(8,128)S(1)}, f32[1024,128]{1,0:T(8,128)S(1)}) custom-call(bf16[128,1024]{1,0:T(8,128)(2,1)S(1)} %collective-permute-done.2.refs_0_, bf16[4,264,128]{2,1,0:T(8,128)(2,1)S(1)} %merge.1.refs_1_.refs_2_, bf16[4,264,128]{2,1,0:T(8,128)(2,1)S(1)} %merge.1.refs_1_.refs_2_, ...), custom_call_target="tpu_custom_call" | custom-call | tf_op jit(solution)/shard_map/attend/pallas_call | solution.py:221
  38.0 5.1 %collective-permute-done.1.refs_0_ = bf16[128,1024]{1,0:T(8,128)(2,1)S(1)} collective-permute-done((bf16[128,1024]{1,0:T(8,128)(2,1)S(1)}, bf16[128,1024]{1,0:T(8,128)(2,1)S(1)}, u32[]{:S(2)}, u32[]{:S(2)}) %collective-permute-start.1) | collective-permute-done | bytes 262176 | tf_op jit(solution)/shard_map/ppermute | solution.py:194
  43.1 1.3 %attend.11 = bf16[128,1024]{1,0:T(8,128)(2,1)S(1)} custom-call(bf16[128,1024]{1,0:T(8,128)(2,1)S(1)} %collective-permute-done.2.refs_0_, bf16[4,264,128]{2,1,0:T(8,128)(2,1)S(1)} %merge.1.refs_1_.refs_2_, bf16[4,264,128]{2,1,0:T(8,128)(2,1)S(1)} %collective-permute-done.9.refs_2_, bf16[4,264,128]{2,1,0:T(8,128)(2,1)S(1)} %collective-permute-done.10.refs_3_, ...), custom_call_target="tpu_custom_call" | custom-call | tf_op jit(solution)/shard_map/attend/pallas_call | solution.py:221
  44.4 4.7 %collective-permute-start.15 = (bf16[128,1024]{1,0:T(8,128)(2,1)S(1)}, bf16[128,1024]{1,0:T(8,128)(2,1)S(1)}, u32[]{:S(2)}, u32[]{:S(2)}) collective-permute-start(bf16[128,1024]{1,0:T(8,128)(2,1)S(1)} %attend.11), channel_id=1, source_target_pairs={{0,24},{8,16},{16,8},{24,0},{1,25},{9,17},{17,9},{25,1},{2,26},{10... | collective-permute-start | bytes 786440 | tf_op jit(solution)/shard_map/ppermute | solution.py:194
  49.1 1.1 %attend.9 = (f32[1024,128]{1,0:T(8,128)S(1)}, f32[1024,128]{1,0:T(8,128)S(1)}, f32[1024,128]{1,0:T(8,128)S(1)}) custom-call(bf16[128,1024]{1,0:T(8,128)(2,1)S(1)} %collective-permute-done.1.refs_0_, bf16[4,264,128]{2,1,0:T(8,128)(2,1)S(1)} %merge.1.refs_1_.refs_2_, bf16[4,264,128]{2,1,0:T(8,128)(2,1)S(1)} %merge.1.refs_1_.refs_2_, ...), custom_call_target="tpu_custom_call" | custom-call | tf_op jit(solution)/shard_map/attend/pallas_call | solution.py:221
  50.2 2.0 %attend.12 = bf16[128,1024]{1,0:T(8,128)(2,1)S(1)} custom-call(bf16[128,1024]{1,0:T(8,128)(2,1)S(1)} %collective-permute-done.1.refs_0_, bf16[4,264,128]{2,1,0:T(8,128)(2,1)S(1)} %merge.1.refs_1_.refs_2_, bf16[4,264,128]{2,1,0:T(8,128)(2,1)S(1)} %collective-permute-done.9.refs_2_, bf16[4,264,128]{2,1,0:T(8,128)(2,1)S(1)} %collective-permute-done.10.refs_3_, ...), custom_call_target="tpu_custom_call" | custom-call | tf_op jit(solution)/shard_map/attend/pallas_call | solution.py:221
  52.2 3.5 %collective-permute-start.14 = (bf16[128,1024]{1,0:T(8,128)(2,1)S(1)}, bf16[128,1024]{1,0:T(8,128)(2,1)S(1)}, u32[]{:S(2)}, u32[]{:S(2)}) collective-permute-start(bf16[128,1024]{1,0:T(8,128)(2,1)S(1)} %attend.12), channel_id=1, source_target_pairs={{0,16},{8,24},{16,0},{24,8},{1,17},{9,25},{17,1},{25,9},{2,18},{10... | collective-permute-start | bytes 786440 | tf_op jit(solution)/shard_map/ppermute | solution.py:194
  55.7 2.6 %attend.10 = (f32[1024,128]{1,0:T(8,128)S(1)}, f32[1024,128]{1,0:T(8,128)S(1)}, f32[1024,128]{1,0:T(8,128)S(1)}) custom-call(bf16[128,1024]{1,0:T(8,128)(2,1)S(1)} %collective-permute-done.refs_0_, bf16[4,264,128]{2,1,0:T(8,128)(2,1)S(1)} %merge.1.refs_1_.refs_2_, bf16[4,264,128]{2,1,0:T(8,128)(2,1)S(1)} %merge.1.refs_1_.refs_2_, ...), custom_call_target="tpu_custom_call" | custom-call | tf_op jit(solution)/shard_map/attend/pallas_call | solution.py:221
  58.3 2.7 %attend.13 = bf16[128,1024]{1,0:T(8,128)(2,1)S(1)} custom-call(bf16[128,1024]{1,0:T(8,128)(2,1)S(1)} %collective-permute-done.refs_0_, bf16[4,264,128]{2,1,0:T(8,128)(2,1)S(1)} %merge.1.refs_1_.refs_2_, bf16[4,264,128]{2,1,0:T(8,128)(2,1)S(1)} %collective-permute-done.9.refs_2_, bf16[4,264,128]{2,1,0:T(8,128)(2,1)S(1)} %collective-permute-done.10.refs_3_, ...), custom_call_target="tpu_custom_call" | custom-call | tf_op jit(solution)/shard_map/attend/pallas_call | solution.py:221
  61.0 2.2 %collective-permute-start.13 = (bf16[128,1024]{1,0:T(8,128)(2,1)S(1)}, bf16[128,1024]{1,0:T(8,128)(2,1)S(1)}, u32[]{:S(2)}, u32[]{:S(2)}) collective-permute-start(bf16[128,1024]{1,0:T(8,128)(2,1)S(1)} %attend.13), channel_id=1, source_target_pairs={{0,8},{8,0},{16,24},{24,16},{1,9},{9,1},{17,25},{25,17},{2,10},{10... | collective-permute-start | bytes 786440 | tf_op jit(solution)/shard_map/ppermute | solution.py:194
  63.1 4.0 %attend.14 = (f32[1024,128]{1,0:T(8,128)S(1)}, f32[1024,128]{1,0:T(8,128)S(1)}, f32[1024,128]{1,0:T(8,128)S(1)}) custom-call(bf16[128,1024]{1,0:T(8,128)(2,1)S(1)} %get-tuple-element.53.refs_0_, bf16[4,264,128]{2,1,0:T(8,128)(2,1)S(1)} %merge.1.refs_1_.refs_2_, bf16[4,264,128]{2,1,0:T(8,128)(2,1)S(1)} %merge.1.refs_1_.refs_2_, ...), custom_call_target="tpu_custom_call" | custom-call | tf_op jit(solution)/shard_map/attend/pallas_call | solution.py:221
  67.1 4.0 %attend.15.refs_0_ = bf16[128,1024]{1,0:T(8,128)(2,1)S(1)} custom-call(bf16[128,1024]{1,0:T(8,128)(2,1)S(1)} %get-tuple-element.53.refs_0_, bf16[4,264,128]{2,1,0:T(8,128)(2,1)S(1)} %merge.1.refs_1_.refs_2_, bf16[4,264,128]{2,1,0:T(8,128)(2,1)S(1)} %collective-permute-done.9.refs_2_, bf16[4,264,128]{2,1,0:T(8,128)(2,1)S(1)} %collective-permute-done.10.refs_3_, ...), custom_call_target="tpu_custom_call" | custom-call | tf_op jit(solution)/shard_map/attend/pallas_call | solution.py:221
  (19 shorter events, 1.8 us)
Async XLA Ops:
  1.4 4.8 %collective-permute-start.3 = (bf16[264,128]{1,0:T(8,128)(2,1)S(1)}, bf16[264,128]{1,0:T(8,128)(2,1)S(1)}, u32[]{:S(2)}, u32[]{:S(2)}) collective-permute-start(bf16[264,128]{1,0:T(8,128)(2,1)S(1)} %get-tuple-element.36), channel_id=1, source_target_pairs={{0,8},{8,0},{16,24},{24,16},{1,9},{9,1},{17,25},{25,17},{2,10},{10... | collective-permute-start | bytes 202760 | tf_op jit(solution)/shard_map/ppermute | solution.py:194
  2.0 5.5 %collective-permute-start.4 = (bf16[264,128]{1,0:T(8,128)(2,1)S(1)}, bf16[264,128]{1,0:T(8,128)(2,1)S(1)}, u32[]{:S(2)}, u32[]{:S(2)}) collective-permute-start(bf16[264,128]{1,0:T(8,128)(2,1)S(1)} %get-tuple-element.37), channel_id=1, source_target_pairs={{0,16},{8,24},{16,0},{24,8},{1,17},{9,25},{17,1},{25,9},{2,18},{10... | collective-permute-start | bytes 202760 | tf_op jit(solution)/shard_map/ppermute | solution.py:194
  2.1 5.5 %collective-permute-start.5 = (bf16[264,128]{1,0:T(8,128)(2,1)S(1)}, bf16[264,128]{1,0:T(8,128)(2,1)S(1)}, u32[]{:S(2)}, u32[]{:S(2)}) collective-permute-start(bf16[264,128]{1,0:T(8,128)(2,1)S(1)} %get-tuple-element.38), channel_id=1, source_target_pairs={{0,24},{8,16},{16,8},{24,0},{1,25},{9,17},{17,9},{25,1},{2,26},{10... | collective-permute-start | bytes 202760 | tf_op jit(solution)/shard_map/ppermute | solution.py:194
  7.5 8.7 %collective-permute-start.6 = (bf16[4,264,128]{2,1,0:T(8,128)(2,1)S(1)}, bf16[4,264,128]{2,1,0:T(8,128)(2,1)S(1)}, u32[]{:S(2)}, u32[]{:S(2)}) collective-permute-start(bf16[4,264,128]{2,1,0:T(8,128)(2,1)S(1)} %merge.1.refs_1_.refs_2_), channel_id=1, source_target_pairs={{0,1},{1,0},{2,3},{3,2},{4,5},{5,4},{6,7},{7,6},{8,9},{9,8},{10,11... | collective-permute-start | bytes 811016 | tf_op jit(solution)/shard_map/ppermute | solution.py:194
  9.4 15.7 %collective-permute-start.10 = (bf16[4,264,128]{2,1,0:T(8,128)(2,1)S(1)}, bf16[4,264,128]{2,1,0:T(8,128)(2,1)S(1)}, u32[]{:S(2)}, u32[]{:S(2)}) collective-permute-start(bf16[4,264,128]{2,1,0:T(8,128)(2,1)S(1)} %merge.1.refs_1_.refs_2_), channel_id=1, source_target_pairs={{0,3},{1,2},{2,1},{3,0},{4,7},{5,6},{6,5},{7,4},{8,11},{9,10},{10,... | collective-permute-start | bytes 811016 | tf_op jit(solution)/shard_map/ppermute | solution.py:194
  11.8 22.5 %collective-permute-start.9 = (bf16[4,264,128]{2,1,0:T(8,128)(2,1)S(1)}, bf16[4,264,128]{2,1,0:T(8,128)(2,1)S(1)}, u32[]{:S(2)}, u32[]{:S(2)}) collective-permute-start(bf16[4,264,128]{2,1,0:T(8,128)(2,1)S(1)} %merge.1.refs_1_.refs_2_), channel_id=1, source_target_pairs={{0,2},{1,3},{2,0},{3,1},{4,6},{5,7},{6,4},{7,5},{8,10},{9,11},{10,... | collective-permute-start | bytes 811016 | tf_op jit(solution)/shard_map/ppermute | solution.py:194
  12.0 23.8 %collective-permute-start.7 = (bf16[4,264,128]{2,1,0:T(8,128)(2,1)S(1)}, bf16[4,264,128]{2,1,0:T(8,128)(2,1)S(1)}, u32[]{:S(2)}, u32[]{:S(2)}) collective-permute-start(bf16[4,264,128]{2,1,0:T(8,128)(2,1)S(1)} %merge.1.refs_1_.refs_2_), channel_id=1, source_target_pairs={{0,4},{4,0},{1,5},{5,1},{2,6},{6,2},{3,7},{7,3},{8,12},{12,8},{9,1... | collective-permute-start | bytes 811016 | tf_op jit(solution)/shard_map/ppermute | solution.py:214
  12.0 22.4 %collective-permute-start.2 = (bf16[128,1024]{1,0:T(8,128)(2,1)S(1)}, bf16[128,1024]{1,0:T(8,128)(2,1)S(1)}, u32[]{:S(2)}, u32[]{:S(2)}) collective-permute-start(bf16[128,1024]{1,0:T(8,128)(2,1)S(1)} %get-tuple-element.34), channel_id=1, source_target_pairs={{0,24},{8,16},{16,8},{24,0},{1,25},{9,17},{17,9},{25,1},{2,26},{10... | collective-permute-start | bytes 786440 | tf_op jit(solution)/shard_map/ppermute | solution.py:194
  16.2 20.6 %collective-permute-start.8 = (bf16[4,264,128]{2,1,0:T(8,128)(2,1)S(1)}, bf16[4,264,128]{2,1,0:T(8,128)(2,1)S(1)}, u32[]{:S(2)}, u32[]{:S(2)}) collective-permute-start(bf16[4,264,128]{2,1,0:T(8,128)(2,1)S(1)} %collective-permute-done.6.refs_3_), channel_id=1, source_target_pairs={{0,4},{4,0},{1,5},{5,1},{2,6},{6,2},{3,7},{7,3},{8,12},{12,8},{9,1... | collective-permute-start | bytes 811016 | tf_op jit(solution)/shard_map/ppermute | solution.py:214
  25.1 18.0 %collective-permute-start.12 = (bf16[4,264,128]{2,1,0:T(8,128)(2,1)S(1)}, bf16[4,264,128]{2,1,0:T(8,128)(2,1)S(1)}, u32[]{:S(2)}, u32[]{:S(2)}) collective-permute-start(bf16[4,264,128]{2,1,0:T(8,128)(2,1)S(1)} %collective-permute-done.10.refs_3_), channel_id=1, source_target_pairs={{0,4},{4,0},{1,5},{5,1},{2,6},{6,2},{3,7},{7,3},{8,12},{12,8},{9,1... | collective-permute-start | bytes 811016 | tf_op jit(solution)/shard_map/ppermute | solution.py:214
  34.4 8.7 %collective-permute-start.11 = (bf16[4,264,128]{2,1,0:T(8,128)(2,1)S(1)}, bf16[4,264,128]{2,1,0:T(8,128)(2,1)S(1)}, u32[]{:S(2)}, u32[]{:S(2)}) collective-permute-start(bf16[4,264,128]{2,1,0:T(8,128)(2,1)S(1)} %collective-permute-done.9.refs_2_), channel_id=1, source_target_pairs={{0,4},{4,0},{1,5},{5,1},{2,6},{6,2},{3,7},{7,3},{8,12},{12,8},{9,1... | collective-permute-start | bytes 811016 | tf_op jit(solution)/shard_map/ppermute | solution.py:214
  34.4 8.7 %collective-permute-start.1 = (bf16[128,1024]{1,0:T(8,128)(2,1)S(1)}, bf16[128,1024]{1,0:T(8,128)(2,1)S(1)}, u32[]{:S(2)}, u32[]{:S(2)}) collective-permute-start(bf16[128,1024]{1,0:T(8,128)(2,1)S(1)} %get-tuple-element.33), channel_id=1, source_target_pairs={{0,16},{8,24},{16,0},{24,8},{1,17},{9,25},{17,1},{25,9},{2,18},{10... | collective-permute-start | bytes 786440 | tf_op jit(solution)/shard_map/ppermute | solution.py:194
  35.8 14.5 %collective-permute-start = (bf16[128,1024]{1,0:T(8,128)(2,1)S(1)}, bf16[128,1024]{1,0:T(8,128)(2,1)S(1)}, u32[]{:S(2)}, u32[]{:S(2)}) collective-permute-start(bf16[128,1024]{1,0:T(8,128)(2,1)S(1)} %get-tuple-element.32), channel_id=1, source_target_pairs={{0,8},{8,0},{16,24},{24,16},{1,9},{9,1},{17,25},{25,17},{2,10},{10... | collective-permute-start | bytes 786440 | tf_op jit(solution)/shard_map/ppermute | solution.py:194
  44.4 26.8 %collective-permute-start.15 = (bf16[128,1024]{1,0:T(8,128)(2,1)S(1)}, bf16[128,1024]{1,0:T(8,128)(2,1)S(1)}, u32[]{:S(2)}, u32[]{:S(2)}) collective-permute-start(bf16[128,1024]{1,0:T(8,128)(2,1)S(1)} %attend.11), channel_id=1, source_target_pairs={{0,24},{8,16},{16,8},{24,0},{1,25},{9,17},{17,9},{25,1},{2,26},{10... | collective-permute-start | bytes 786440 | tf_op jit(solution)/shard_map/ppermute | solution.py:194
  52.2 19.0 %collective-permute-start.14 = (bf16[128,1024]{1,0:T(8,128)(2,1)S(1)}, bf16[128,1024]{1,0:T(8,128)(2,1)S(1)}, u32[]{:S(2)}, u32[]{:S(2)}) collective-permute-start(bf16[128,1024]{1,0:T(8,128)(2,1)S(1)} %attend.12), channel_id=1, source_target_pairs={{0,16},{8,24},{16,0},{24,8},{1,17},{9,25},{17,1},{25,9},{2,18},{10... | collective-permute-start | bytes 786440 | tf_op jit(solution)/shard_map/ppermute | solution.py:194
  61.0 10.2 %collective-permute-start.13 = (bf16[128,1024]{1,0:T(8,128)(2,1)S(1)}, bf16[128,1024]{1,0:T(8,128)(2,1)S(1)}, u32[]{:S(2)}, u32[]{:S(2)}) collective-permute-start(bf16[128,1024]{1,0:T(8,128)(2,1)S(1)} %attend.13), channel_id=1, source_target_pairs={{0,8},{8,0},{16,24},{24,16},{1,9},{9,1},{17,25},{25,17},{2,10},{10... | collective-permute-start | bytes 786440 | tf_op jit(solution)/shard_map/ppermute | solution.py:194
